TPU v7x, 256 devices: a whole 4x4x8 slice. The times are simulated.
256 devices in a mesh: wa: 64 (over x_hi, y, z), ba: 4 (over x_lo, core).
Axes of the slice: x: 4 (x_hi: 2, x_lo: 2; x = x_hi * 2 + x_lo), y: 4, z: 8, core: 2. Of those that a mesh axis runs over, the one named last changes fastest.
Arguments:
- latent: float32 [16, 8, 8192], P('ba', None, 'wa'), parts along dimension 0, may hold values from -12 to 12
- noise: float32 [2, 16, 8, 8192], P(None, 'ba', None, 'wa'), parts along dimension 1, may hold values from -6 to 6
- offsets: int32 [128], P('wa'), may hold values from 0 to 63
- anchors: int32 [2], replicated, may hold values from 0 to 127
- guidance: float32 [1], replicated, may hold values from 0.4 to 0.8
- w_in: bfloat16 [320, 36], replicated, may hold values from -1 to 1
- w_mid: bfloat16 [320, 320], replicated, may hold values from -0.3125 to 0.3125
- w_out: bfloat16 [36, 320], replicated, may hold values from -0.109375 to 0.109375
- t_embed: float32 [2, 320], replicated, may hold values from -6 to 6
- w_feat: float32 [64, 4], replicated, may hold values from -3 to 3
Outputs:
- denoised: float32 [16, 8, 8192], P('ba', None, 'wa'), parts along dimension 0
There are 4 independent parts, one for each index of `ba`. A program takes and returns all parts, laid end to end along the dimension named above; an argument that names none is the same for every part. Nothing has to cross between parts.
All inputs are finite; a program needn't handle non-finite values.
Results may differ from a plain program's by a relative error of at most 0.0065.
Values sent between devices are 32-bit elements; how exact they have to be, the bound alone decides.
No kernel may reach another device: no remote copies, remote signals or barrier semaphores. Data moves between devices by JAX's collectives and lax.ppermute only.
A program may use at most 64 MiB of HBM per device.

v0:
```python
import math

import jax
import jax.numpy as jnp
from jax import lax
from jax.sharding import Mesh
from jax.sharding import PartitionSpec as P

WIN = 128
STRIDE = 64
STEPS = 2
WA = ("wa_0", "wa_1", "wa_2")


TAP_SHIFTS = ((-1, -1), (-1, 0), (-1, 1), (0, -1), (0, 0), (0, 1), (1, -1), (1, 0), (1, 1))
CUMULATIVE_ALPHA = (0.35, 0.55, 0.72, 0.85, 0.93)
STABILITY = 1e-06


def broadcast_by_axis(shard, axes, root):
    shard = jnp.where(lax.axis_index(axes) == root, shard, jnp.zeros_like(shard))
    for axis in axes:
        shard = lax.psum(shard, axis)
    return shard


def from_everyone(shard, axis):
    copies = jnp.broadcast_to(shard, (lax.axis_size(axis), *shard.shape))
    return lax.all_to_all(copies, axis, split_axis=0, concat_axis=0, tiled=True)


def of_everyone(shard, axis):
    return from_everyone(shard, axis).sum(axis=0)


def passed_along(shard, axis, by):
    length = lax.axis_size(axis)
    return lax.ppermute(shard, axis, [(i, (i + by) % length) for i in range(length)])


def plan(number):
    current = CUMULATIVE_ALPHA[number]
    following = CUMULATIVE_ALPHA[number + 1]
    spread = 0.3 * math.sqrt(1.0 - following)
    return (
        math.sqrt(current),
        math.sqrt(1.0 - current),
        math.sqrt(following),
        math.sqrt(1.0 - following - spread * spread),
        spread,
    )


def tapped(field):
    height, columns = (field.shape[-2], field.shape[-1])
    padding = [(0, 0)] * (field.ndim - 2) + [(1, 1), (1, 1)]
    padded = jnp.pad(field, padding)
    return jnp.stack(
        [
            padded[..., 1 + down_by : 1 + down_by + height, 1 + right_by : 1 + right_by + columns]
            for down_by, right_by in TAP_SHIFTS
        ]
    )


def denoise(window, w_in, w_mid, w_out, embedding):
    channels, height, columns = window.shape
    stacked = tapped(window.astype(jnp.bfloat16)).reshape(9 * channels, height * columns)
    hidden_in = jnp.dot(w_in, stacked, preferred_element_type=jnp.float32) + embedding[:, None]
    activated = jax.nn.silu(hidden_in).astype(jnp.bfloat16)
    middle = jnp.dot(w_mid, activated, preferred_element_type=jnp.float32)
    joined = (hidden_in + jax.nn.silu(middle)).astype(jnp.bfloat16)
    outward = jnp.dot(w_out, joined, preferred_element_type=jnp.float32).reshape(
        9, channels, height, columns
    )
    padded = jnp.pad(outward, ((0, 0), (0, 0), (1, 1), (1, 1)))
    result = jnp.zeros((channels, height, columns), jnp.float32)
    for index, (down_by, right_by) in enumerate(TAP_SHIFTS):
        result = (
            result
            + padded[
                index, :, 1 + down_by : 1 + down_by + height, 1 + right_by : 1 + right_by + columns
            ]
        )
    return result


def clean_of(windows, w_in, w_mid, w_out, embedding, now_a, now_s):
    predicted = jax.vmap(denoise, (0, None, None, None, None))(
        windows, w_in, w_mid, w_out, embedding
    )
    cleaned = (windows - now_s * predicted) / now_a
    return (cleaned, predicted)


def percept(cleaned, w_feat):
    return jax.nn.silu(jnp.einsum("fc,chw->fhw", w_feat, cleaned, precision=lax.Precision.HIGHEST))


def mismatch(cleaned, anchor_percept, w_feat):
    difference = percept(cleaned, w_feat) - anchor_percept
    return 0.5 * jnp.sum(difference * difference) / w_feat.shape[0]


def finish_gradient(cleaned, pullback, anchor_percept, w_feat):
    clean_grad = jax.vmap(jax.grad(mismatch), (0, None, None))(cleaned, anchor_percept, w_feat)
    return pullback(clean_grad)[0]


def advance(windows, gradient, predicted, scale, now_a, now_s, next_a, direction):
    return next_a * (windows - scale * gradient - now_s * predicted) / now_a + direction * predicted


def window_update(extended, number, starts, anchors, guidance, w_in, w_mid, w_out, t_embed, w_feat):
    per_dev = starts.shape[0]
    now_a, now_s, next_a, direction, spread = plan(number)
    embedding = t_embed[number]
    windows = jnp.stack(
        [lax.dynamic_slice_in_dim(extended, starts[index], WIN, 2) for index in range(per_dev)]
    )

    def cleaning(inputs):
        return clean_of(inputs, w_in, w_mid, w_out, embedding, now_a, now_s)

    cleaned, pullback, predicted = jax.vjp(cleaning, windows, has_aux=True)
    owner = anchors[number] // per_dev
    slot = anchors[number] % per_dev
    picked = lax.dynamic_index_in_dim(cleaned, slot, 0, keepdims=False)
    anchor_percept = percept(broadcast_by_axis(picked, WA, owner), w_feat)
    gradient = finish_gradient(cleaned, pullback, anchor_percept, w_feat)
    square_sum = of_everyone(jnp.sum(gradient * gradient), WA)
    element_count = per_dev * lax.axis_size(WA) * windows.shape[1] * windows.shape[2] * WIN
    scale = guidance[0] * lax.rsqrt(square_sum / element_count + STABILITY)
    advanced = advance(windows, gradient, predicted, scale, now_a, now_s, next_a, direction)
    summed = jnp.zeros(extended.shape, jnp.float32)
    for index in range(per_dev):
        current = lax.dynamic_slice_in_dim(summed, starts[index], WIN, 2)
        summed = lax.dynamic_update_slice_in_dim(
            summed, current + advanced[index], starts[index], 2
        )
    return (summed, spread)


def local(latent, noise, offsets, anchors, guidance, w_in, w_mid, w_out, t_embed, w_feat):
    width = latent.shape[-1]
    per_dev = offsets.shape[0]
    starts = jnp.arange(per_dev, dtype=jnp.int32) * STRIDE + offsets
    positions = jnp.arange(2 * width, dtype=jnp.int32)
    inside = (positions[None, :] >= starts[:, None]) & (positions[None, :] < starts[:, None] + WIN)
    cover = jnp.sum(inside.astype(jnp.float32), axis=0)
    count_own = cover[:width] + passed_along(cover[width:], WA, 1)
    state = latent
    for number in range(STEPS):
        neighbour = passed_along(state, WA, -1)
        extended = jnp.concatenate([state, neighbour], axis=2)
        summed, spread = window_update(
            extended, number, starts, anchors, guidance, w_in, w_mid, w_out, t_embed, w_feat
        )
        spill = passed_along(summed[:, :, width:], WA, 1)
        state = (summed[:, :, :width] + spill) / count_own + spread * noise[number]
    return state


def solution(mesh):
    finer = Mesh(mesh.devices.reshape(2, 4, 8, mesh.shape["ba"]), ("wa_0", "wa_1", "wa_2", "ba"))
    placed = (P("ba", None, WA), P(None, "ba", None, WA), P(WA), P(), P(), P(), P(), P(), P(), P())
    return jax.shard_map(
        local, mesh=finer, in_specs=placed, out_specs=P("ba", None, WA), check_vma=False
    )
```

profile of v0, /device:TPU:2, one launch (start us, length us, event | category | flops | bytes accessed | tf_op | source)
XLA Modules:
  0.0 238.8 jit_solution(6218011149825673397)
XLA Ops:
  0.8 9.9 %collective-permute-start = (f32[4,8,128]{2,0,1:T(4,128)S(1)}, f32[4,8,128]{2,0,1:T(4,128)S(1)}, u32[]{:S(2)}, u32[]{:S(2)}) collective-permute-start(f32[4,8,128]{2,0,1:T(4,128)S(1)} %get-tuple-element.43), channel_id=1, source_target_pairs={{0,252},{4,0},{8,4},{12,8},{16,12},{20,16},{24,20},{28,24},{32,28}... | collective-permute-start | bytes 49160 | tf_op jit(solution)/shard_map/ppermute | solution.py:38
  12.6 1.4 slice_reduce_fusion
  13.9 1.4 fusion.240
  22.8 1.3 fusion.190
  24.1 2.6 %fusion.88 = f32[2,1024,320]{1,2,0:T(8,128)} fusion(f32[2,1024,320]{1,2,0:T(8,128)S(1)} %fusion.190, f32[320]{0:T(512)S(1)} %get-tuple-element.6, bf16[320,320]{1,0:T(8,128)(2,1)S(1)} %copy-done), kind=kOutput, calls=%fused_computation.107 | convolution fusion | flops 423362560 | bytes 5448960 | tf_op jit(solution)/shard_map/jvp(vmap())/dot_general | solution.py:71
  26.7 2.6 %fusion.94 = f32[2,36,1024]{2,1,0:T(8,128)S(1)} fusion(f32[2,1024,320]{1,2,0:T(8,128)} %fusion.88, f32[2,1024,320]{1,2,0:T(8,128)S(1)} %fusion.190, f32[320]{0:T(512)S(1)} %get-tuple-element.6, bf16[36,320]{1,0:T(8,128)(2,1)S(1)} %copy-done.3), kind=kOutput, calls=%fused_computation.112 | convolution fusion | flops 51773440 | bytes 5562112 | tf_op jit(solution)/shard_map/jvp(vmap())/dot_general | solution.py:73
  29.7 9.6 %psum.42 = f32[4,8,128]{2,0,1:T(4,128)S(1)} all-reduce(f32[4,8,128]{2,0,1:T(4,128)S(1)} %select_bitcast_fusion.1), channel_id=1, replica_groups=mesh['wa_0'=2,'wa_1'=4,'wa_2'=8,'ba'=4] {'wa_0'}, use_global_device_ids=true, to_apply=%region_0.0 | all-reduce | flops 4096 | bytes 32768 | tf_op jit(solution)/shard_map/psum | solution.py:23
  39.2 14.3 %psum.43 = f32[4,8,128]{2,0,1:T(4,128)S(1)} all-reduce(f32[4,8,128]{2,0,1:T(4,128)S(1)} %psum.42), channel_id=1, replica_groups=mesh['wa_0'=2,'wa_1'=4,'wa_2'=8,'ba'=4] {'wa_1'}, use_global_device_ids=true, to_apply=%region_1.2 | all-reduce | flops 4096 | bytes 32768 | tf_op jit(solution)/shard_map/psum | solution.py:23
  53.5 34.2 %psum.44 = f32[4,8,128]{2,0,1:T(4,128)S(1)} all-reduce(f32[4,8,128]{2,0,1:T(4,128)S(1)} %psum.43), channel_id=1, replica_groups=mesh['wa_0'=2,'wa_1'=4,'wa_2'=8,'ba'=4] {'wa_2'}, use_global_device_ids=true, to_apply=%region_2.3 | all-reduce | flops 4096 | bytes 32768 | tf_op jit(solution)/shard_map/psum | solution.py:23
  87.7 1.3 convolution_bitcast_fusion.1
  89.0 1.1 divide_multiply_fusion.1
  91.4 1.6 convolution_convert_fusion.1
  93.0 5.1 %fusion.110 = bf16[2,36,1024]{2,1,0:T(8,128)(2,1)S(1)} fusion(bf16[2,1024,320]{1,2,0:T(8,128)(2,1)} %convolution_convert_fusion.1, f32[2,1024,320]{1,2,0:T(8,128)S(1)} %fusion.190, f32[2,1024,320]{1,2,0:T(8,128)} %fusion.88, f32[320]{0:T(512)S(1)} %copy-done.13, bf16[320,320]{1,0:T(8,128)(2,1)S(1)} %copy-done, bf16[320,36]{0,1:T(8,128)(2,1)S(1)} %copy-done.1), kind=kOutput, calls=%fused_computation.118 | convolution fusion | flops 482418688 | bytes 6930176 | tf_op jit(solution)/shard_map/transpose(jvp(vmap()))/dot_general | solution.py:69
  99.2 1.3 broadcast_in_dim.9
  100.4 4.8 %all-to-all-start = ((f32[64,1,1]{2,1,0:T(1,128)}), f32[64,1,1]{2,1,0:T(1,128)S(1)}, u32[]{:S(2)}, u32[]{:S(2)}) async-start(f32[64,1,1]{2,1,0:T(1,128)} %broadcast_in_dim.9), calls=%async_computation | async-start | bytes 65536 | tf_op jit(solution)/shard_map/all_to_all | solution.py:29
  106.5 10.6 %all-to-all-done = f32[64,1,1]{2,1,0:T(1,128)S(1)} async-done(((f32[64,1,1]{2,1,0:T(1,128)}), f32[64,1,1]{2,1,0:T(1,128)S(1)}, u32[]{:S(2)}, u32[]{:S(2)}) %all-to-all-start) | async-done | bytes 288 | tf_op jit(solution)/shard_map/all_to_all | solution.py:29
  118.5 1.3 dynamic_update_slice.12
  119.9 1.3 dynamic_update_slice.13
  122.5 8.3 %collective-permute-done.1 = f32[4,8,128]{2,0,1:T(4,128)S(1)} collective-permute-done((f32[4,8,128]{2,0,1:T(4,128)S(1)}, f32[4,8,128]{2,0,1:T(4,128)S(1)}, u32[]{:S(2)}, u32[]{:S(2)}) %collective-permute-start.1) | collective-permute-done | bytes 16416 | tf_op jit(solution)/shard_map/ppermute | solution.py:38
  133.4 1.2 collective-permute-done.3
  137.2 1.5 copy-done.16
  140.0 1.3 convolution_bitcast_fusion
  141.3 8.9 %psum.45 = f32[4,8,128]{2,0,1:T(4,128)S(1)} all-reduce(f32[4,8,128]{2,0,1:T(4,128)S(1)} %select_bitcast_fusion), channel_id=1, replica_groups=mesh['wa_0'=2,'wa_1'=4,'wa_2'=8,'ba'=4] {'wa_0'}, use_global_device_ids=true, to_apply=%region_6.7 | all-reduce | flops 4096 | bytes 32768 | tf_op jit(solution)/shard_map/psum | solution.py:23
  150.2 14.3 %psum.46 = f32[4,8,128]{2,0,1:T(4,128)S(1)} all-reduce(f32[4,8,128]{2,0,1:T(4,128)S(1)} %psum.45), channel_id=1, replica_groups=mesh['wa_0'=2,'wa_1'=4,'wa_2'=8,'ba'=4] {'wa_1'}, use_global_device_ids=true, to_apply=%region_7.8 | all-reduce | flops 4096 | bytes 32768 | tf_op jit(solution)/shard_map/psum | solution.py:23
  164.5 32.8 %psum.47 = f32[4,8,128]{2,0,1:T(4,128)S(1)} all-reduce(f32[4,8,128]{2,0,1:T(4,128)S(1)} %psum.46), channel_id=1, replica_groups=mesh['wa_0'=2,'wa_1'=4,'wa_2'=8,'ba'=4] {'wa_2'}, use_global_device_ids=true, to_apply=%region_8.9 | all-reduce | flops 4096 | bytes 32768 | tf_op jit(solution)/shard_map/psum | solution.py:23
  198.5 1.3 fusion.120
  200.4 1.6 convolution_convert_fusion
  202.1 5.1 %fusion.115 = bf16[2,36,1024]{2,1,0:T(8,128)(2,1)S(1)} fusion(bf16[2,1024,320]{1,2,0:T(8,128)(2,1)} %convolution_convert_fusion, f32[2,1024,320]{1,2,0:T(8,128)S(1)} %fusion.187, f32[2,1024,320]{1,2,0:T(8,128)} %copy-done.16, f32[320]{0:T(512)S(1)} %copy-done.11, bf16[320,320]{1,0:T(8,128)(2,1)S(1)} %copy-done, bf16[320,36]{0,1:T(8,128)(2,1)S(1)} %copy-done.2), kind=kOutput, calls=%fused_computation.119 | convolution fusion | flops 482418688 | bytes 6930176 | tf_op jit(solution)/shard_map/transpose(jvp(vmap()))/dot_general | solution.py:69
  208.8 15.8 %all_to_all.12 = f32[64,1,1]{2,1,0:T(1,128)S(1)} all-to-all(f32[64,1,1]{2,1,0:T(1,128)S(1)} %broadcast_in_dim.11), channel_id=1, replica_groups=mesh['wa_0'=2,'wa_1'=4,'wa_2'=8,'ba'=4] {'wa_0','wa_1','wa_2'}, dimensions={0} | all-to-all | bytes 512 | tf_op jit(solution)/shard_map/all_to_all | solution.py:29
  225.9 1.3 dynamic_update_slice.14
  227.3 1.3 dynamic_update_slice.15
  229.4 8.8 %collective-permute-done.4 = f32[4,8,128]{2,0,1:T(4,128)S(1)} collective-permute-done((f32[4,8,128]{2,0,1:T(4,128)S(1)}, f32[4,8,128]{2,0,1:T(4,128)S(1)}, u32[]{:S(2)}, u32[]{:S(2)}) %collective-permute-start.4) | collective-permute-done | bytes 16416 | tf_op jit(solution)/shard_map/ppermute | solution.py:38
  (124 shorter events, 18.1 us)
Async XLA Ops:
  0.0 24.1 %copy-start = (bf16[320,320]{1,0:T(8,128)(2,1)S(1)}, bf16[320,320]{1,0:T(8,128)(2,1)}, u32[]{:S(2)}) copy-start(bf16[320,320]{1,0:T(8,128)(2,1)} %param.16) | copy-start | bytes 614404
  0.8 21.1 %collective-permute-start = (f32[4,8,128]{2,0,1:T(4,128)S(1)}, f32[4,8,128]{2,0,1:T(4,128)S(1)}, u32[]{:S(2)}, u32[]{:S(2)}) collective-permute-start(f32[4,8,128]{2,0,1:T(4,128)S(1)} %get-tuple-element.43), channel_id=1, source_target_pairs={{0,252},{4,0},{8,4},{12,8},{16,12},{20,16},{24,20},{28,24},{32,28}... | collective-permute-start | bytes 49160 | tf_op jit(solution)/shard_map/ppermute | solution.py:38
  11.4 1.2 copy-start.14
  12.0 110.0 %collective-permute-start.2 = (f32[128]{0:T(128)}, f32[128]{0:T(128)}, u32[]{:S(2)}, u32[]{:S(2)}) collective-permute-start(f32[128]{0:T(128)} %slice.200), channel_id=1, source_target_pairs={{0,4},{4,8},{8,12},{12,16},{16,20},{20,24},{24,28},{28,32},{32,36}... | collective-permute-start | bytes 1544 | tf_op jit(solution)/shard_map/ppermute | solution.py:38
  13.9 12.7 %copy-start.12 = (f32[320]{0:T(512)}, f32[320]{0:T(512)S(1)}, u32[]{:S(2)}) copy-start(f32[320]{0:T(512)S(1)} %get-tuple-element.6) | copy-start | bytes 3844
  24.1 2.6 %copy-start.3 = (bf16[36,320]{1,0:T(8,128)(2,1)S(1)}, bf16[36,320]{1,0:T(8,128)(2,1)}, u32[]{:S(2)}) copy-start(bf16[36,320]{1,0:T(8,128)(2,1)} %param.17) | copy-start | bytes 69124
  29.4 60.8 %copy-start.7 = (f32[64,4]{0,1:T(4,128)S(1)}, f32[64,4]{0,1:T(4,128)}, u32[]{:S(2)}) copy-start(f32[64,4]{0,1:T(4,128)} %param.19) | copy-start | bytes 3076
  90.2 2.9 %copy-start.1 = (bf16[320,36]{0,1:T(8,128)(2,1)S(1)}, bf16[320,36]{0,1:T(8,128)(2,1)}, u32[]{:S(2)}) copy-start(bf16[320,36]{0,1:T(8,128)(2,1)} %param.15) | copy-start | bytes 69124
  90.2 2.8 %copy-start.13 = (f32[320]{0:T(512)S(1)}, f32[320]{0:T(512)}, u32[]{:S(2)}) copy-start(f32[320]{0:T(512)} %copy-done.12) | copy-start | bytes 3844
  93.0 12.2 %copy-start.6 = (f32[2,4,8,128]{3,2,1,0:T(8,128)S(1)}, f32[2,4,8,128]{3,2,1,0:T(8,128)}, u32[]{:S(2)}) copy-start(f32[2,4,8,128]{3,2,1,0:T(8,128)} %param.11) | copy-start | bytes 98308
  93.0 28.9 %copy-start.15 = (f32[256]{0:T(256)S(1)}, f32[256]{0:T(256)}, u32[]{:S(2)}) copy-start(f32[256]{0:T(256)} %copy-done.14) | copy-start | bytes 3076
  98.3 37.9 %copy-start.10 = (f32[320]{0:T(512)S(1)}, f32[320]{0:T(512)}, u32[]{:S(2)}) copy-start(f32[320]{0:T(512)} %get-tuple-element.5) | copy-start | bytes 3844
  100.4 16.6 %all-to-all-start = ((f32[64,1,1]{2,1,0:T(1,128)}), f32[64,1,1]{2,1,0:T(1,128)S(1)}, u32[]{:S(2)}, u32[]{:S(2)}) async-start(f32[64,1,1]{2,1,0:T(1,128)} %broadcast_in_dim.9), calls=%async_computation | async-start | bytes 65536 | tf_op jit(solution)/shard_map/all_to_all | solution.py:29
  121.2 9.5 %collective-permute-start.1 = (f32[4,8,128]{2,0,1:T(4,128)S(1)}, f32[4,8,128]{2,0,1:T(4,128)S(1)}, u32[]{:S(2)}, u32[]{:S(2)}) collective-permute-start(f32[4,8,128]{2,0,1:T(4,128)S(1)} %slice.230), channel_id=1, source_target_pairs={{0,4},{4,8},{8,12},{12,16},{16,20},{20,24},{24,28},{28,32},{32,36}... | collective-permute-start | bytes 49160 | tf_op jit(solution)/shard_map/ppermute | solution.py:38
  122.5 10.9 %copy-start.8 = (f32[128]{0:T(128)}, f32[128]{0:T(128)S(1)}, u32[]{:S(2)}) copy-start(f32[128]{0:T(128)S(1)} %slice_add_fusion.2) | copy-start | bytes 1540
  130.8 3.8 %collective-permute-start.3 = (f32[4,8,128]{2,0,1:T(4,128)S(1)}, f32[4,8,128]{2,0,1:T(4,128)S(1)}, u32[]{:S(2)}, u32[]{:S(2)}) collective-permute-start(f32[4,8,128]{2,0,1:T(4,128)S(1)} %divide_add_fusion.1), channel_id=1, source_target_pairs={{0,252},{4,0},{8,4},{12,8},{16,12},{20,16},{24,20},{28,24},{32,28}... | collective-permute-start | bytes 49160 | tf_op jit(solution)/shard_map/ppermute | solution.py:38
  137.2 1.5 copy-start.16
  198.5 1.9 copy-start.4
  198.5 3.6 %copy-start.2 = (bf16[320,36]{0,1:T(8,128)(2,1)S(1)}, bf16[320,36]{0,1:T(8,128)(2,1)}, u32[]{:S(2)}) copy-start(bf16[320,36]{0,1:T(8,128)(2,1)} %param.15) | copy-start | bytes 69124
  199.8 2.2 copy-start.11
  202.0 36.1 %copy-start.5 = (f32[1,4,8,128]{3,2,1,0:T(8,128)S(1)}, f32[1,4,8,128]{3,2,1,0:T(8,128)}, u32[]{:S(2)}) copy-start(f32[1,4,8,128]{3,2,1,0:T(8,128)} %get-tuple-element.42) | copy-start | bytes 49156
  202.0 36.1 %copy-start.9 = (f32[128]{0:T(128)S(1)}, f32[128]{0:T(128)}, u32[]{:S(2)}) copy-start(f32[128]{0:T(128)} %copy-done.8) | copy-start | bytes 1540
  228.6 9.5 %collective-permute-start.4 = (f32[4,8,128]{2,0,1:T(4,128)S(1)}, f32[4,8,128]{2,0,1:T(4,128)S(1)}, u32[]{:S(2)}, u32[]{:S(2)}) collective-permute-start(f32[4,8,128]{2,0,1:T(4,128)S(1)} %slice.235), channel_id=1, source_target_pairs={{0,4},{4,8},{8,12},{12,16},{16,20},{20,24},{24,28},{28,32},{32,36}... | collective-permute-start | bytes 49160 | tf_op jit(solution)/shard_map/ppermute | solution.py:38
where the time goes:
time: 240 us; the launch traced here: 239 us
  blocking collectives  130 us (54%)
  matrix products  29.2 us (12%)
  waiting for transfers between devices  28.9 us (12%)
  local copies, waits for them, and re-layouts  16.4 us (7%)
  starting transfers between devices  16.1 us (7%)
  between operations  11.6 us (5%)
  other arithmetic  6.67 us (3%)
    psum x6, blocking collectives, broadcast_by_axis(): shard = lax.psum(shard, axis)  114 us
    ppermute x5, waiting for transfers between devices, passed_along(): lax.ppermute(shard, axis, [(i, (i + by) % length) for i in range(length)])  18.3 us
    all_to_all x1, blocking collectives, from_everyone(): return lax.all_to_all(copies, axis, split_axis=0, concat_axis=0, tiled=True)  15.8 us
    dot_general x4, matrix products, denoise(): jnp.dot(w_in, stacked, preferred_element_type=jnp.float32)  12 us
    ppermute x5, starting transfers between devices, passed_along(): lax.ppermute(shard, axis, [(i, (i + by) % length) for i in range(length)])  11.3 us
    all_to_all x1, waiting for transfers between devices, from_everyone(): return lax.all_to_all(copies, axis, split_axis=0, concat_axis=0, tiled=True)  10.6 us
    dot_general x6, matrix products, percept(): jnp.einsum('fc,chw->fhw', w_feat, cleaned, precision=lax.Precision.HIGHEST)  6.83 us
    dot_general x4, matrix products, denoise(): jnp.dot(w_out, joined, preferred_element_type=jnp.float32)  6.8 us
  transfers between devices with their start and end apart: 6, of which 4 were waited for; matrix products, arithmetic and copies ran while one was open for 12% of the time, Pallas kernels for 0%

commit v1 on v0

v1 whole, which is shorter than its diff:
```python
import functools
import math

import jax
import jax.numpy as jnp
from jax import lax
from jax.experimental import pallas as pl
from jax.experimental.pallas import tpu as pltpu
from jax.sharding import Mesh
from jax.sharding import PartitionSpec as P

C = 4
H = 8
HID = 320
FEAT = 64
WIN = 128
STRIDE = 64
NDEV = 64
NWIN = 128
TAPS = 9 * C
FIELD = H * WIN
CHUNK = 512
WA = ("wa_0", "wa_1", "wa_2")
NEAR = "wa_2"
FAR = ("wa_0", "wa_1")
GROUP = 8

TAP_SHIFTS = ((-1, -1), (-1, 0), (-1, 1), (0, -1), (0, 0), (0, 1), (1, -1), (1, 0), (1, 1))
CUMULATIVE_ALPHA = (0.35, 0.55, 0.72, 0.85, 0.93)
STABILITY = 1e-06
ELEMENTS = float(NWIN * C * H * WIN)
F32 = jnp.float32
BF16 = jnp.bfloat16


def plan(number):
    current = CUMULATIVE_ALPHA[number]
    following = CUMULATIVE_ALPHA[number + 1]
    spread = 0.3 * math.sqrt(1.0 - following)
    return (
        math.sqrt(current),
        math.sqrt(1.0 - current),
        math.sqrt(following),
        math.sqrt(1.0 - following - spread * spread),
        spread,
    )


def lanes(shape=(C, H, WIN)):
    return lax.broadcasted_iota(jnp.int32, shape, len(shape) - 1)


def shift_rows(x, by):
    if by == 0:
        return x
    row = lax.broadcasted_iota(jnp.int32, x.shape, 1)
    inside = row >= 1 if by < 0 else row < H - 1
    return jnp.where(inside, pltpu.roll(x, (-by) % H, 1), 0.0)


def shift_lanes(x, by):
    if by == 0:
        return x
    lane = lanes(x.shape)
    inside = lane >= 1 if by < 0 else lane < WIN - 1
    return jnp.where(inside, pltpu.roll(x, (-by) % WIN, 2), 0.0)


def spread_taps(x, sign, tall):
    moved = {by: shift_lanes(x, sign * by) for by in (-1, 0, 1)}
    for k, (down, right) in enumerate(TAP_SHIFTS):
        tall[32 * k : 32 * (k + 1), :] = shift_rows(moved[right], sign * down).reshape(32, WIN)
    rows = [tall[pl.ds(h, TAPS, stride=H), :] for h in range(H)]
    return jnp.concatenate(rows, axis=1).astype(BF16)


def store_taps(tall, first, values):
    for j in range(values.shape[1] // WIN):
        tall[pl.ds(first + j, TAPS, stride=H), :] = values[:, WIN * j : WIN * (j + 1)]


def gather_taps(tall, sign):
    total = None
    for right in (-1, 0, 1):
        part = None
        for k, (down, across) in enumerate(TAP_SHIFTS):
            if across == right:
                piece = tall[32 * k : 32 * (k + 1), :].reshape(C, H, WIN)
                piece = shift_rows(piece, sign * down)
                part = piece if part is None else part + piece
        part = shift_lanes(part, sign * right)
        total = part if total is None else total + part
    return total


def silu_and_slope(v):
    u = 0.5 * v
    t = jnp.tanh(u)
    s = u + u * t
    g = 0.5 + 0.5 * t
    return s, g + s * (1.0 - g)


def silu(v):
    u = 0.5 * v
    return u + u * jnp.tanh(u)


def dot(a, b):
    return lax.dot_general(a, b, (((1,), (0,)), ((), ())), preferred_element_type=F32)


def predict(window, weights, embed, tall, slopes, slot):
    taps = spread_taps(window, 1, tall)
    for start in range(0, FIELD, CHUNK):
        hidden = dot(weights["w_in"][...], taps[:, start : start + CHUNK]) + embed
        if slopes is None:
            active = silu(hidden)
            joined = hidden + silu(dot(weights["w_mid"][...], active.astype(BF16)))
        else:
            at = pl.ds(slot * FIELD + start, CHUNK)
            active, slopes[0][:, at] = silu_and_slope(hidden)
            more, slopes[1][:, at] = silu_and_slope(dot(weights["w_mid"][...], active.astype(BF16)))
            joined = hidden + more
        store_taps(tall, start // WIN, dot(weights["w_out"][...], joined.astype(BF16)))
    return gather_taps(tall, 1)


def pull_back(cotangent, weights, tall, slopes, slot):
    taps = spread_taps(cotangent, -1, tall)
    for start in range(0, FIELD, CHUNK):
        at = pl.ds(slot * FIELD + start, CHUNK)
        d_joined = dot(weights["w_out_t"][...], taps[:, start : start + CHUNK])
        d_middle = (d_joined * slopes[1][:, at]).astype(BF16)
        d_hidden = d_joined + dot(weights["w_mid_t"][...], d_middle) * slopes[0][:, at]
        store_taps(tall, start // WIN, dot(weights["w_in_t"][...], d_hidden.astype(BF16)))
    return gather_taps(tall, -1)


def percept_pull_back(cleans, anchor, w_feat):
    grads = [[jnp.zeros((H, WIN), F32) for _ in range(C)] for _ in cleans]
    for f in range(FEAT):
        w = [w_feat[f * C + c] for c in range(C)]

        def mixed(x):
            return (w[0] * x[0] + w[1] * x[1]) + (w[2] * x[2] + w[3] * x[3])

        target = silu(mixed(anchor))
        for x, grad in zip(cleans, grads):
            s, slope = silu_and_slope(mixed(x))
            d = (s - target) * slope
            for c in range(C):
                grad[c] = grad[c] + w[c] * d
    return [jnp.stack(grad) * (1.0 / FEAT) for grad in grads]


def cut(first, second, start):
    by = (WIN - start) % WIN
    return jnp.where(
        lanes() < WIN - start, pltpu.roll(first, by, 2), pltpu.roll(second, by, 2)
    )


def place(pieces, starts):
    own, spill = 0.0, 0.0
    for piece, start in zip(pieces, starts):
        moved = pltpu.roll(piece, start, 2)
        inside = lanes() >= start
        own = own + jnp.where(inside, moved, 0.0)
        spill = spill + jnp.where(inside, 0.0, moved)
    return own, spill


def step(number, first, second, starts, anchor, weights, embed_ref, w_feat, scratch):
    now_a, now_s, next_a, direction, _ = plan(number)
    talls, slopes = scratch[:3], scratch[3:]
    embed = jnp.broadcast_to(embed_ref[:, number : number + 1], (HID, CHUNK))
    windows = [cut(first, second, start) for start in starts]
    predicted = [
        predict(windows[i], weights, embed, talls[i], slopes, i) for i in range(2)
    ]
    anchor_predicted = predict(anchor, weights, embed, talls[2], None, 2)
    cleans = [(w - now_s * p) * (1.0 / now_a) for w, p in zip(windows, predicted)]
    anchor_clean = (anchor - now_s * anchor_predicted) * (1.0 / now_a)
    d_cleans = percept_pull_back(cleans, anchor_clean, w_feat)
    gradients = [
        d * (1.0 / now_a)
        + pull_back(d * (-now_s / now_a), weights, talls[i], slopes, i)
        for i, d in enumerate(d_cleans)
    ]
    square = sum(jnp.sum(g * g, axis=0) for g in gradients)
    plain = [
        (next_a / now_a) * (w - now_s * p) + direction * p for w, p in zip(windows, predicted)
    ]
    plain_own, plain_spill = place(plain, starts)
    steep_own, steep_spill = place([g * (-next_a / now_a) for g in gradients], starts)
    return plain_own, plain_spill, steep_own, steep_spill, square


def scale_of(total, guidance):
    return guidance[0] * lax.rsqrt(jnp.full((1, 1, 1), total) * (1.0 / ELEMENTS) + STABILITY)


def opening_kernel(me_ref, anchors, offsets, latent, noise, share, halo):
    me = me_ref[0]
    owner = anchors[0] // 2
    own = latent[...]
    x = jnp.where(me == owner, own, 0.0)
    y = jnp.where(me == (owner + 1) % NDEV, own, 0.0)
    lane = lanes((H, WIN))
    known = jnp.where(
        lane == 2 * me,
        offsets[0].astype(F32),
        jnp.where(lane == 2 * me + 1, offsets[1].astype(F32), 0.0),
    )
    for i in range(GROUP):
        share[i, 0:4] = x
        share[i, 4:8] = y
        share[i, 8] = known
    halo[0:4] = own
    halo[4:8] = noise[0]


def relay_kernel(got, share):
    total = got[0]
    for i in range(1, GROUP):
        total = total + got[i]
    for i in range(GROUP):
        share[i] = total


def weights_of(refs):
    names = ("w_in", "w_mid", "w_out", "w_in_t", "w_mid_t", "w_out_t")
    return dict(zip(names, refs))


def first_kernel(
    me_ref, anchors, offsets, w_feat, latent, noise, halo, shared,
    w_in, w_mid, w_out, w_in_t, w_mid_t, w_out_t, embed,
    share, own_out, spill_out, inverse, *scratch,
):
    weights = weights_of((w_in, w_mid, w_out, w_in_t, w_mid_t, w_out_t))
    me = me_ref[0]
    total = shared[0]
    for i in range(1, GROUP):
        total = total + shared[i]
    table = total[8]
    lane = lanes((H, WIN))

    def offset_of(window):
        picked = jnp.where(lane == window, table, 0.0)[0:1]
        return jnp.sum(picked).astype(jnp.int32)

    starts = (offsets[0], STRIDE + offsets[1])
    anchor_at = (anchors[0] % 2) * STRIDE + offset_of(anchors[0])
    anchor = cut(total[0:4], total[4:8], anchor_at)
    plain_own, plain_spill, steep_own, steep_spill, square = step(
        0, latent[...], halo[0:4], starts, anchor, weights, embed, w_feat, scratch
    )
    spread = plan(0)[-1]

    def covered(windows):
        count = jnp.zeros((H, WIN), F32)
        for begin in windows:
            count = count + jnp.where((lane >= begin) & (lane < begin + WIN), 1.0, 0.0)
        return 1.0 / count

    left, right = 2 * me + NWIN - 2, 2 * me + 2
    before = (
        offset_of(left % NWIN) - WIN,
        offset_of((left + 1) % NWIN) - STRIDE,
    )
    after = (offset_of(right % NWIN), STRIDE + offset_of((right + 1) % NWIN))
    inverse_own = covered(before + starts)
    inverse_next = covered((starts[0] - WIN, starts[1] - WIN) + after)
    inverse[0] = inverse_own
    inverse[1] = inverse_next
    own_out[0:4] = plain_own
    own_out[4:8] = steep_own
    spill_out[0:4] = plain_spill
    spill_out[4:8] = steep_spill

    owner = anchors[1] // 2
    next_at = (anchors[1] % 2) * STRIDE + offset_of(anchors[1])
    here, ahead, behind = (
        me == owner, me == (owner + 1) % NDEV, me == (owner + NDEV - 1) % NDEV
    )

    def portion(own, spill):
        x = jnp.where(here, own, jnp.where(behind, spill, 0.0))
        y = jnp.where(here, spill, jnp.where(ahead, own, 0.0))
        return cut(x, y, next_at)

    plain_part = portion(
        plain_own * inverse_own + spread * noise[0], plain_spill * inverse_next
    )
    steep_part = portion(steep_own * inverse_own, steep_spill * inverse_next)
    for i in range(GROUP):
        share[i, 0:4] = plain_part
        share[i, 4:8] = steep_part
        share[i, 8] = square


def second_kernel(
    offsets, w_feat, guidance, noise, halo, shared, own_in, spill_in, spill_left, own_right, inverse,
    w_in, w_mid, w_out, w_in_t, w_mid_t, w_out_t, embed,
    own_out, spill_out, square_out, *scratch,
):
    weights = weights_of((w_in, w_mid, w_out, w_in_t, w_mid_t, w_out_t))
    total = shared[0]
    for i in range(1, GROUP):
        total = total + shared[i]
    scale = scale_of(jnp.sum(total[8]), guidance)
    spread = plan(0)[-1]
    anchor = total[0:4] + scale * total[4:8]
    own = own_in[...] + spill_left[...]
    beyond = spill_in[...] + own_right[...]
    first = (own[0:4] + scale * own[4:8]) * inverse[0] + spread * noise[0]
    second = (beyond[0:4] + scale * beyond[4:8]) * inverse[1] + spread * halo[4:8]
    starts = (offsets[0], STRIDE + offsets[1])
    plain_own, plain_spill, steep_own, steep_spill, square = step(
        1, first, second, starts, anchor, weights, embed, w_feat, scratch
    )
    own_out[0:4] = plain_own
    own_out[4:8] = steep_own
    spill_out[0:4] = plain_spill
    spill_out[4:8] = steep_spill
    row = jnp.sum(square, axis=0, keepdims=True)
    square_out[...] = jnp.broadcast_to(row[None], (NDEV, 1, WIN))


def closing_kernel(guidance, squares, own_in, spill_left, inverse, noise, out):
    scale = scale_of(jnp.sum(squares[...]), guidance)
    own = own_in[...] + spill_left[...]
    spread = plan(1)[-1]
    out[...] = (own[0:4] + scale * own[4:8]) * inverse[0] + spread * noise[1]


def call(kernel, shapes, n_scalars, *args, scratch=()):
    in_specs = [
        pl.BlockSpec(memory_space=pltpu.SMEM if i < n_scalars else pltpu.VMEM)
        for i in range(len(args))
    ]
    return pl.pallas_call(
        kernel,
        out_shape=[jax.ShapeDtypeStruct(shape, F32) for shape in shapes],
        in_specs=in_specs,
        out_specs=[pl.BlockSpec(memory_space=pltpu.VMEM) for _ in shapes],
        scratch_shapes=scratch,
        name=kernel.__name__,
    )(*args)


def scratches():
    return [pltpu.VMEM((8 * TAPS, WIN), F32)] * 3 + [pltpu.VMEM((HID, 2 * FIELD), F32)] * 2


def exchanged(shares, axes):
    return lax.all_to_all(shares, axes, split_axis=0, concat_axis=0, tiled=True)


def passed_along(shard, by):
    return lax.ppermute(shard, WA, [(i, (i + by) % NDEV) for i in range(NDEV)])


def local(latent, noise, offsets, anchors, guidance, w_in, w_mid, w_out, t_embed, w_feat):
    me = lax.axis_index(WA).astype(jnp.int32).reshape(1)
    features = w_feat.reshape(-1)
    weights = (w_in, w_mid, w_out, w_in.T, w_mid.T, w_out.T, t_embed.T)
    blocks, group = (8, H, WIN), (GROUP, 9, H, WIN)

    share, halo = call(opening_kernel, (group, blocks), 3, me, anchors, offsets, latent, noise)
    halo = passed_along(halo, -1)
    (share,) = call(relay_kernel, (group,), 0, exchanged(share, NEAR))
    share = exchanged(share, FAR)

    share, own, spill, inverse = call(
        first_kernel, (group, blocks, blocks, (2, H, WIN)), 4,
        me, anchors, offsets, features, latent, noise, halo, share, *weights,
        scratch=scratches(),
    )
    spill_left = passed_along(spill, 1)
    own_right = passed_along(own, -1)
    (share,) = call(relay_kernel, (group,), 0, exchanged(share, NEAR))
    share = exchanged(share, FAR)

    own, spill, squares = call(
        second_kernel, (blocks, blocks, (NDEV, 1, WIN)), 3,
        offsets, features, guidance, noise, halo, share, own, spill, spill_left, own_right,
        inverse, *weights,
        scratch=scratches(),
    )
    spill_left = passed_along(spill, 1)
    squares = exchanged(squares, WA)
    (out,) = call(
        closing_kernel, ((C, H, WIN),), 1, guidance, squares, own, spill_left, inverse, noise
    )
    return out


def solution(mesh):
    finer = Mesh(mesh.devices.reshape(2, 4, 8, mesh.shape["ba"]), ("wa_0", "wa_1", "wa_2", "ba"))
    placed = (P("ba", None, WA), P(None, "ba", None, WA), P(WA), P(), P(), P(), P(), P(), P(), P())
    return jax.shard_map(
        local, mesh=finer, in_specs=placed, out_specs=P("ba", None, WA), check_vma=False
    )
```

time: 240 us -> 118 us (0.49)
  blocking collectives: 130 us -> 36 us
  matrix products: 29.2 us -> 0 us
  Pallas kernels: 0 us -> 26.1 us
  starting transfers between devices: 16.1 us -> 28.3 us
  between operations: 11.6 us -> 0.73 us
  local copies, waits for them, and re-layouts: 16.4 us -> 6.01 us
  waiting for transfers between devices: 28.9 us -> 19.5 us
  other arithmetic: 6.67 us -> 0 us
    psum x6 -> x0, blocking collectives: 114 us -> none  [broadcast_by_axis(): shard = lax.psum(shard, axis)]
    dot_general x16 -> x0, matrix products: 29.2 us -> none  [the longest x4 12 us: denoise(): jnp.dot(w_in, stacked, preferred_element_type=jnp.float32)]
    pallas_call x0 -> x6, Pallas kernels: none -> 26.1 us  [call(): pl.pallas_call(kernel, out_shape=[jax.ShapeDtypeStruct(shape, F32) for sh...]
    all_to_all x1 -> x2, blocking collectives: 15.8 us -> 36 us  [exchanged(): return lax.all_to_all(shares, axes, split_axis=0, concat_axis=0, tiled=True)]
    all_to_all x1 -> x3, starting transfers between devices: 4.77 us -> 15.9 us  [exchanged(): return lax.all_to_all(shares, axes, split_axis=0, concat_axis=0, tiled=True)]
    all_to_all x1 -> x3, waiting for transfers between devices: 10.6 us -> 2.36 us  [exchanged(): return lax.all_to_all(shares, axes, split_axis=0, concat_axis=0, tiled=True)]
    dynamic_update_slice x4 -> x0, local copies, waits for them, and re-layouts: 5.25 us -> none  [window_update(): lax.dynamic_update_slice_in_dim(summed, current + advanced[index], starts...]
    slice x6 -> x0, local copies, waits for them, and re-layouts: 3.92 us -> none  [the longest x1 1.37 us: window_update(): embedding = t_embed[number]]
  transfers between devices with their start and end apart: 6 -> 7, of which waited for: 4 -> 4; matrix products, arithmetic and copies ran while one was open for 12% -> 3% of each run, Pallas kernels for 0% -> 0%
where the time goes in v1:
time: 118 us; the launch traced here: 117 us
  blocking collectives  36 us (31%)
  starting transfers between devices  28.3 us (24%)
  Pallas kernels  26.1 us (22%)
  waiting for transfers between devices  19.5 us (17%)
  local copies, waits for them, and re-layouts  6.01 us (5%)
    all_to_all x2, blocking collectives, exchanged(): return lax.all_to_all(shares, axes, split_axis=0, concat_axis=0, tiled=True)  36 us
    pallas_call x6, Pallas kernels, call(): pl.pallas_call(kernel, out_shape=[jax.ShapeDtypeStruct(shape, F32) for sh...  26.1 us
    ppermute x4, waiting for transfers between devices, passed_along(): return lax.ppermute(shard, WA, [(i, (i + by) % NDEV) for i in range(NDEV)])  17.2 us
    all_to_all x3, starting transfers between devices, exchanged(): return lax.all_to_all(shares, axes, split_axis=0, concat_axis=0, tiled=True)  15.9 us
    ppermute x4, starting transfers between devices, passed_along(): return lax.ppermute(shard, WA, [(i, (i + by) % NDEV) for i in range(NDEV)])  12.4 us
    unnamed x37, local copies, waits for them, and re-layouts  5.34 us
  transfers between devices with their start and end apart: 7, of which 4 were waited for; matrix products, arithmetic and copies ran while one was open for 3% of the time, Pallas kernels for 0%

profile of v1, /device:TPU:2, one launch (start us, length us, event | category | flops | bytes accessed | tf_op | source)
XLA Modules:
  0.0 116.8 jit_solution(15339237039802321973)
XLA Ops:
  0.0 1.5 %opening_kernel.1 = (f32[8,9,8,128]{3,2,1,0:T(8,128)}, f32[8,8,128]{2,1,0:T(8,128)}) custom-call(s32[1]{0:T(128)} %bitcast.me_ref, s32[2]{0:T(128)} %anchors.3, s32[2]{0:T(128)} %offsets.5, f32[4,8,128]{2,1,0:T(8,128)} %latent.3, f32[2,4,8,128]{3,2,1,0:T(8,128)} %noise.7), custom_call_target="tpu_custom_call" | custom-call | tf_op jit(solution)/shard_map/opening_kernel/pallas_call | solution.py:344
  1.5 21.1 %all_to_all.25.got = f32[8,9,8,128]{3,2,1,0:T(8,128)} all-to-all(f32[8,9,8,128]{3,2,1,0:T(8,128)} %get-tuple-element.15), channel_id=1, replica_groups=mesh['wa_0'=2,'wa_1'=4,'wa_2'=8,'ba'=4] {'wa_2'}, dimensions={0} | all-to-all | bytes 589824 | tf_op jit(solution)/shard_map/all_to_all | solution.py:359
  22.7 1.7 %relay_kernel.2 = f32[8,9,8,128]{3,2,1,0:T(8,128)} custom-call(f32[8,9,8,128]{3,2,1,0:T(8,128)} %all_to_all.25.got), custom_call_target="tpu_custom_call" | custom-call | tf_op jit(solution)/shard_map/relay_kernel/pallas_call | solution.py:344
  24.4 6.2 %all-to-all-start.1 = ((f32[8,9,8,128]{3,2,1,0:T(8,128)}), f32[8,9,8,128]{3,2,1,0:T(8,128)S(1)}, u32[]{:S(2)}, u32[]{:S(2)}) async-start(f32[8,9,8,128]{3,2,1,0:T(8,128)} %relay_kernel.2), calls=%async_computation.1 | async-start | bytes 589824 | tf_op jit(solution)/shard_map/all_to_all | solution.py:359
  30.6 5.5 %collective-permute-start = (f32[8,8,128]{2,1,0:T(8,128)S(1)}, f32[8,8,128]{2,1,0:T(8,128)S(1)}, u32[]{:S(2)}, u32[]{:S(2)}) collective-permute-start(f32[8,8,128]{2,1,0:T(8,128)S(1)} %copy-done.15), channel_id=1, source_target_pairs={{0,252},{4,0},{8,4},{12,8},{16,12},{20,16},{24,20},{28,24},{32,28}... | collective-permute-start | bytes 98312 | tf_op jit(solution)/shard_map/ppermute | solution.py:363
  36.1 0.1 copy.16
  36.2 0.7 reshape.6.w_feat
  36.9 0.7 copy.20.w_in
  37.6 0.7 copy.18
  38.3 0.8 copy.19
  39.2 0.9 copy.17
  40.0 0.0 collective-permute-done.halo
  40.0 0.6 copy-done.5
  40.6 0.1 copy-done.2
  40.8 9.8 %first_kernel.1 = (f32[8,9,8,128]{3,2,1,0:T(8,128)}, f32[8,8,128]{2,1,0:T(8,128)}, f32[8,8,128]{2,1,0:T(8,128)}, f32[2,8,128]{2,1,0:T(8,128)}) custom-call(s32[1]{0:T(128)} %bitcast.me_ref, s32[2]{0:T(128)} %anchors.3, s32[2]{0:T(128)} %offsets.5, f32[256]{0:T(256)} %reshape.6.w_feat, f32[4,8,128]{2,1,0:T(8,128)} %latent.3, f32[2,4,8,128]{3,2,1,0:T(8,128)} %noise.7, ...), custom_call_target="tpu_custom_call" | custom-call | tf_op jit(solution)/shard_map/first_kernel/pallas_call | solution.py:344
  50.5 14.9 %all_to_all.26.got = f32[8,9,8,128]{3,2,1,0:T(8,128)} all-to-all(f32[8,9,8,128]{3,2,1,0:T(8,128)} %get-tuple-element.16), channel_id=1, replica_groups=mesh['wa_0'=2,'wa_1'=4,'wa_2'=8,'ba'=4] {'wa_2'}, dimensions={0} | all-to-all | bytes 589824 | tf_op jit(solution)/shard_map/all_to_all | solution.py:359
  65.4 1.7 %relay_kernel.3 = f32[8,9,8,128]{3,2,1,0:T(8,128)} custom-call(f32[8,9,8,128]{3,2,1,0:T(8,128)} %all_to_all.26.got), custom_call_target="tpu_custom_call" | custom-call | tf_op jit(solution)/shard_map/relay_kernel/pallas_call | solution.py:344
  67.1 5.0 %all-to-all-start.3 = ((f32[8,9,8,128]{3,2,1,0:T(8,128)}), f32[8,9,8,128]{3,2,1,0:T(8,128)S(1)}, u32[]{:S(2)}, u32[]{:S(2)}) async-start(f32[8,9,8,128]{3,2,1,0:T(8,128)} %relay_kernel.3), calls=%async_computation.3 | async-start | bytes 589824 | tf_op jit(solution)/shard_map/all_to_all | solution.py:359
  72.1 5.4 %collective-permute-start.2 = (f32[8,8,128]{2,1,0:T(8,128)S(1)}, f32[8,8,128]{2,1,0:T(8,128)S(1)}, u32[]{:S(2)}, u32[]{:S(2)}) collective-permute-start(f32[8,8,128]{2,1,0:T(8,128)S(1)} %copy-done.7), channel_id=1, source_target_pairs={{0,252},{4,0},{8,4},{12,8},{16,12},{20,16},{24,20},{28,24},{32,28}... | collective-permute-start | bytes 98312 | tf_op jit(solution)/shard_map/ppermute | solution.py:363
  77.5 0.0 collective-permute-start.1
  78.2 0.9 collective-permute-done.2.own_right
  79.1 8.0 %collective-permute-done.1.spill_left = f32[8,8,128]{2,1,0:T(8,128)S(1)} collective-permute-done((f32[8,8,128]{2,1,0:T(8,128)S(1)}, f32[8,8,128]{2,1,0:T(8,128)S(1)}, u32[]{:S(2)}, u32[]{:S(2)}) %collective-permute-start.1) | collective-permute-done | bytes 32800 | tf_op jit(solution)/shard_map/ppermute | solution.py:363
  87.2 0.0 all-to-all-done.3.shared
  87.2 0.6 copy-done.10
  87.8 0.1 copy-done.1
  87.9 9.8 %second_kernel.1 = (f32[8,8,128]{2,1,0:T(8,128)}, f32[8,8,128]{2,1,0:T(8,128)}, f32[64,1,128]{2,1,0:T(1,128)}) custom-call(s32[2]{0:T(128)} %offsets.5, f32[256]{0:T(256)} %reshape.6.w_feat, f32[1]{0:T(128)S(6)} %copy.22.guidance, f32[2,4,8,128]{3,2,1,0:T(8,128)} %noise.7, f32[8,8,128]{2,1,0:T(8,128)} %copy-done.5, f32[8,9,8,128]{3,2,1,0:T(8,128)} %copy-done.1, ...), custom_call_target="tpu_custom_call" | custom-call | tf_op jit(solution)/shard_map/second_kernel/pallas_call | solution.py:344
  97.7 4.7 %all-to-all-start.4 = ((f32[64,1,128]{2,1,0:T(1,128)}), f32[64,1,128]{2,1,0:T(1,128)S(1)}, u32[]{:S(2)}, u32[]{:S(2)}) async-start(f32[64,1,128]{2,1,0:T(1,128)} %get-tuple-element.20), calls=%async_computation.4 | async-start | bytes 65536 | tf_op jit(solution)/shard_map/all_to_all | solution.py:359
  102.4 1.5 %collective-permute-start.3 = (f32[8,8,128]{2,1,0:T(8,128)S(1)}, f32[8,8,128]{2,1,0:T(8,128)S(1)}, u32[]{:S(2)}, u32[]{:S(2)}) collective-permute-start(f32[8,8,128]{2,1,0:T(8,128)S(1)} %copy-done.14), channel_id=1, source_target_pairs={{0,4},{4,8},{8,12},{12,16},{16,20},{20,24},{24,28},{28,32},{32,36}... | collective-permute-start | bytes 98312 | tf_op jit(solution)/shard_map/ppermute | solution.py:363
  104.0 8.2 %collective-permute-done.3.spill_left = f32[8,8,128]{2,1,0:T(8,128)S(1)} collective-permute-done((f32[8,8,128]{2,1,0:T(8,128)S(1)}, f32[8,8,128]{2,1,0:T(8,128)S(1)}, u32[]{:S(2)}, u32[]{:S(2)}) %collective-permute-start.3) | collective-permute-done | bytes 32800 | tf_op jit(solution)/shard_map/ppermute | solution.py:363
  112.2 2.4 %all-to-all-done.4.squares = f32[64,1,128]{2,1,0:T(1,128)S(1)} async-done(((f32[64,1,128]{2,1,0:T(1,128)}), f32[64,1,128]{2,1,0:T(1,128)S(1)}, u32[]{:S(2)}, u32[]{:S(2)}) %all-to-all-start.4) | async-done | bytes 32800 | tf_op jit(solution)/shard_map/all_to_all | solution.py:359
  114.5 0.6 copy-done.6
  115.1 1.6 %closing_kernel.1 = f32[4,8,128]{2,1,0:T(8,128)} custom-call(f32[1]{0:T(128)S(6)} %copy.22.guidance, f32[64,1,128]{2,1,0:T(1,128)} %copy-done.6, f32[8,8,128]{2,1,0:T(8,128)} %get-tuple-element.21.own_in, f32[8,8,128]{2,1,0:T(8,128)} %copy-done.11, f32[2,8,128]{2,1,0:T(8,128)} %get-tuple-element.19.inverse, f32[2,4,8,128]{3,2,1,0:T(8,128)} %noise.7), custom_call_target="tpu_custom_call" | custom-call | tf_op jit(solution)/shard_map/closing_kernel/pallas_call | solution.py:344
  (28 shorter events, 0.1 us)
Async XLA Ops:
  24.4 6.2 %copy-start.15 = (f32[8,8,128]{2,1,0:T(8,128)S(1)}, f32[8,8,128]{2,1,0:T(8,128)}, u32[]{:S(2)}) copy-start(f32[8,8,128]{2,1,0:T(8,128)} %get-tuple-element.14) | copy-start | bytes 98308
  24.4 11.7 %copy-start.13 = (f32[64,4]{0,1:T(4,128)S(1)}, f32[64,4]{0,1:T(4,128)}, u32[]{:S(2)}) copy-start(f32[64,4]{0,1:T(4,128)} %param.19) | copy-start | bytes 3076
  24.4 12.4 %copy-start.3 = (bf16[320,36]{0,1:T(8,128)(2,1)S(1)}, bf16[320,36]{0,1:T(8,128)(2,1)}, u32[]{:S(2)}) copy-start(bf16[320,36]{0,1:T(8,128)(2,1)} %param.15) | copy-start | bytes 69124
  24.4 13.2 %copy-start.4 = (bf16[36,320]{1,0:T(8,128)(2,1)S(1)}, bf16[36,320]{1,0:T(8,128)(2,1)}, u32[]{:S(2)}) copy-start(bf16[36,320]{1,0:T(8,128)(2,1)} %w_out.3) | copy-start | bytes 69124
  24.4 15.6 %all-to-all-start.1 = ((f32[8,9,8,128]{3,2,1,0:T(8,128)}), f32[8,9,8,128]{3,2,1,0:T(8,128)S(1)}, u32[]{:S(2)}, u32[]{:S(2)}) async-start(f32[8,9,8,128]{3,2,1,0:T(8,128)} %relay_kernel.2), calls=%async_computation.1 | async-start | bytes 589824 | tf_op jit(solution)/shard_map/all_to_all | solution.py:359
  30.6 8.6 %copy-start = (bf16[320,320]{1,0:T(8,128)(2,1)S(1)}, bf16[320,320]{1,0:T(8,128)(2,1)}, u32[]{:S(2)}) copy-start(bf16[320,320]{1,0:T(8,128)(2,1)} %w_mid.3) | copy-start | bytes 614404
  30.6 9.4 %collective-permute-start = (f32[8,8,128]{2,1,0:T(8,128)S(1)}, f32[8,8,128]{2,1,0:T(8,128)S(1)}, u32[]{:S(2)}, u32[]{:S(2)}) collective-permute-start(f32[8,8,128]{2,1,0:T(8,128)S(1)} %copy-done.15), channel_id=1, source_target_pairs={{0,252},{4,0},{8,4},{12,8},{16,12},{20,16},{24,20},{28,24},{32,28}... | collective-permute-start | bytes 98312 | tf_op jit(solution)/shard_map/ppermute | solution.py:363
  37.6 0.7 copy-start.12
  40.0 0.6 copy-start.5
  40.0 0.7 copy-start.2
  67.1 5.0 %copy-start.7 = (f32[8,8,128]{2,1,0:T(8,128)S(1)}, f32[8,8,128]{2,1,0:T(8,128)}, u32[]{:S(2)}) copy-start(f32[8,8,128]{2,1,0:T(8,128)} %get-tuple-element.17.own_in) | copy-start | bytes 98308
  67.1 10.4 %copy-start.8 = (f32[8,8,128]{2,1,0:T(8,128)S(1)}, f32[8,8,128]{2,1,0:T(8,128)}, u32[]{:S(2)}) copy-start(f32[8,8,128]{2,1,0:T(8,128)} %get-tuple-element.18.spill_in) | copy-start | bytes 98308
  67.1 20.1 %all-to-all-start.3 = ((f32[8,9,8,128]{3,2,1,0:T(8,128)}), f32[8,9,8,128]{3,2,1,0:T(8,128)S(1)}, u32[]{:S(2)}, u32[]{:S(2)}) async-start(f32[8,9,8,128]{3,2,1,0:T(8,128)} %relay_kernel.3), calls=%async_computation.3 | async-start | bytes 589824 | tf_op jit(solution)/shard_map/all_to_all | solution.py:359
  72.1 7.0 %collective-permute-start.2 = (f32[8,8,128]{2,1,0:T(8,128)S(1)}, f32[8,8,128]{2,1,0:T(8,128)S(1)}, u32[]{:S(2)}, u32[]{:S(2)}) collective-permute-start(f32[8,8,128]{2,1,0:T(8,128)S(1)} %copy-done.7), channel_id=1, source_target_pairs={{0,252},{4,0},{8,4},{12,8},{16,12},{20,16},{24,20},{28,24},{32,28}... | collective-permute-start | bytes 98312 | tf_op jit(solution)/shard_map/ppermute | solution.py:363
  77.5 9.6 %collective-permute-start.1 = (f32[8,8,128]{2,1,0:T(8,128)S(1)}, f32[8,8,128]{2,1,0:T(8,128)S(1)}, u32[]{:S(2)}, u32[]{:S(2)}) collective-permute-start(f32[8,8,128]{2,1,0:T(8,128)S(1)} %copy-done.8), channel_id=1, source_target_pairs={{0,4},{4,8},{8,12},{12,16},{16,20},{20,24},{24,28},{28,32},{32,36}... | collective-permute-start | bytes 98312 | tf_op jit(solution)/shard_map/ppermute | solution.py:363
  79.1 8.1 %copy-start.9 = (f32[8,8,128]{2,1,0:T(8,128)}, f32[8,8,128]{2,1,0:T(8,128)S(1)}, u32[]{:S(2)}) copy-start(f32[8,8,128]{2,1,0:T(8,128)S(1)} %collective-permute-done.2.own_right) | copy-start | bytes 98308
  87.2 0.6 copy-start.10
  87.2 0.7 copy-start.1
  97.7 4.7 %copy-start.14 = (f32[8,8,128]{2,1,0:T(8,128)S(1)}, f32[8,8,128]{2,1,0:T(8,128)}, u32[]{:S(2)}) copy-start(f32[8,8,128]{2,1,0:T(8,128)} %get-tuple-element.22) | copy-start | bytes 98308
  97.7 16.8 %all-to-all-start.4 = ((f32[64,1,128]{2,1,0:T(1,128)}), f32[64,1,128]{2,1,0:T(1,128)S(1)}, u32[]{:S(2)}, u32[]{:S(2)}) async-start(f32[64,1,128]{2,1,0:T(1,128)} %get-tuple-element.20), calls=%async_computation.4 | async-start | bytes 65536 | tf_op jit(solution)/shard_map/all_to_all | solution.py:359
  102.4 9.7 %collective-permute-start.3 = (f32[8,8,128]{2,1,0:T(8,128)S(1)}, f32[8,8,128]{2,1,0:T(8,128)S(1)}, u32[]{:S(2)}, u32[]{:S(2)}) collective-permute-start(f32[8,8,128]{2,1,0:T(8,128)S(1)} %copy-done.14), channel_id=1, source_target_pairs={{0,4},{4,8},{8,12},{12,16},{16,20},{20,24},{24,28},{28,32},{32,36}... | collective-permute-start | bytes 98312 | tf_op jit(solution)/shard_map/ppermute | solution.py:363
  112.2 2.4 %copy-start.11 = (f32[8,8,128]{2,1,0:T(8,128)}, f32[8,8,128]{2,1,0:T(8,128)S(1)}, u32[]{:S(2)}) copy-start(f32[8,8,128]{2,1,0:T(8,128)S(1)} %collective-permute-done.3.spill_left) | copy-start | bytes 98308
  114.5 0.6 copy-start.6

commit v2 on v1

--- a/solution.py
+++ b/solution.py
@@ -1,4 +1,3 @@
-import functools
 import math
 
 import jax
@@ -336,7 +335,7 @@
     out[...] = (own[0:4] + scale * own[4:8]) * inverse[0] + spread * noise[1]
 
 
-def call(kernel, shapes, n_scalars, *args, scratch=()):
+def call(kernel, shapes, n_scalars, *args, scratch=(), megabytes=4):
     in_specs = [
         pl.BlockSpec(memory_space=pltpu.SMEM if i < n_scalars else pltpu.VMEM)
         for i in range(len(args))
@@ -347,7 +346,7 @@
         in_specs=in_specs,
         out_specs=[pl.BlockSpec(memory_space=pltpu.VMEM) for _ in shapes],
         scratch_shapes=scratch,
-        name=kernel.__name__,
+        compiler_params=pltpu.CompilerParams(vmem_limit_bytes=megabytes << 20),
     )(*args)
 
 
@@ -371,24 +370,26 @@
 
     share, halo = call(opening_kernel, (group, blocks), 3, me, anchors, offsets, latent, noise)
     halo = passed_along(halo, -1)
-    (share,) = call(relay_kernel, (group,), 0, exchanged(share, NEAR))
+    share = exchanged(share, NEAR)
+    (share,) = call(relay_kernel, (group,), 0, share)
     share = exchanged(share, FAR)
 
     share, own, spill, inverse = call(
         first_kernel, (group, blocks, blocks, (2, H, WIN)), 4,
         me, anchors, offsets, features, latent, noise, halo, share, *weights,
-        scratch=scratches(),
+        scratch=scratches(), megabytes=24,
     )
     spill_left = passed_along(spill, 1)
     own_right = passed_along(own, -1)
-    (share,) = call(relay_kernel, (group,), 0, exchanged(share, NEAR))
+    share = exchanged(share, NEAR)
+    (share,) = call(relay_kernel, (group,), 0, share)
     share = exchanged(share, FAR)
 
     own, spill, squares = call(
         second_kernel, (blocks, blocks, (NDEV, 1, WIN)), 3,
         offsets, features, guidance, noise, halo, share, own, spill, spill_left, own_right,
         inverse, *weights,
-        scratch=scratches(),
+        scratch=scratches(), megabytes=24,
     )
     spill_left = passed_along(spill, 1)
     squares = exchanged(squares, WA)

time: 118 us -> 110 us (0.932)
  Pallas kernels: 26.1 us -> 20 us
  local copies, waits for them, and re-layouts: 6.01 us -> 2.84 us
  waiting for transfers between devices: 19.5 us -> 21.6 us
  blocking collectives: 36 us -> 34 us
  starting transfers between devices: 28.3 us -> 29.9 us
    pallas_call x6, Pallas kernels: 26.1 us -> 20 us  [call(): pl.pallas_call(kernel, out_shape=[jax.ShapeDtypeStruct(shape, F32) for sh...]
    unnamed x37 -> x25, local copies, waits for them, and re-layouts: 5.34 us -> 2.74 us
    all_to_all x2, blocking collectives: 36 us -> 34 us  [exchanged(): return lax.all_to_all(shares, axes, split_axis=0, concat_axis=0, tiled=True)]
    all_to_all x3, waiting for transfers between devices: 2.36 us -> 4.21 us  [exchanged(): return lax.all_to_all(shares, axes, split_axis=0, concat_axis=0, tiled=True)]
    all_to_all x3, starting transfers between devices: 15.9 us -> 17.5 us  [exchanged(): return lax.all_to_all(shares, axes, split_axis=0, concat_axis=0, tiled=True)]
  transfers between devices with their start and end apart: 7 -> 7, of which waited for: 4 -> 6; matrix products, arithmetic and copies ran while one was open for 3% -> 1% of each run, Pallas kernels for 0% -> 0%
where the time goes in v2:
time: 110 us; the launch traced here: 109 us
  blocking collectives  34 us (31%)
  starting transfers between devices  29.9 us (27%)
  waiting for transfers between devices  21.6 us (20%)
  Pallas kernels  20 us (18%)
  local copies, waits for them, and re-layouts  2.84 us (3%)
    all_to_all x2, blocking collectives, exchanged(): return lax.all_to_all(shares, axes, split_axis=0, concat_axis=0, tiled=True)  34 us
    pallas_call x6, Pallas kernels, call(): pl.pallas_call(kernel, out_shape=[jax.ShapeDtypeStruct(shape, F32) for sh...  20 us
    all_to_all x3, starting transfers between devices, exchanged(): return lax.all_to_all(shares, axes, split_axis=0, concat_axis=0, tiled=True)  17.5 us
    ppermute x4, waiting for transfers between devices, passed_along(): return lax.ppermute(shard, WA, [(i, (i + by) % NDEV) for i in range(NDEV)])  17.4 us
    ppermute x4, starting transfers between devices, passed_along(): return lax.ppermute(shard, WA, [(i, (i + by) % NDEV) for i in range(NDEV)])  12.4 us
    all_to_all x3, waiting for transfers between devices, exchanged(): return lax.all_to_all(shares, axes, split_axis=0, concat_axis=0, tiled=True)  4.21 us
    unnamed x25, local copies, waits for them, and re-layouts  2.74 us
  transfers between devices with their start and end apart: 7, of which 6 were waited for; matrix products, arithmetic and copies ran while one was open for 1% of the time, Pallas kernels for 0%

profile of v2, /device:TPU:2, one launch (start us, length us, event | category | flops | bytes accessed | tf_op | source)
XLA Modules:
  0.0 109.0 jit_solution(14268347960647983203)
XLA Ops:
  0.0 0.7 copy-done.5
  0.7 0.8 copy-done.1
  1.5 0.6 shard_map.100
  2.1 20.8 %all_to_all.25.got = f32[8,9,8,128]{3,2,1,0:T(8,128)S(1)} all-to-all(f32[8,9,8,128]{3,2,1,0:T(8,128)S(1)} %get-tuple-element.15), channel_id=1, replica_groups=mesh['wa_0'=2,'wa_1'=4,'wa_2'=8,'ba'=4] {'wa_2'}, dimensions={0} | all-to-all | bytes 589824 | tf_op jit(solution)/shard_map/all_to_all | solution.py:358
  22.9 0.7 shard_map.101
  23.7 6.2 %all-to-all-start.1 = ((f32[8,9,8,128]{3,2,1,0:T(8,128)}), f32[8,9,8,128]{3,2,1,0:T(8,128)S(1)}, u32[]{:S(2)}, u32[]{:S(2)}) async-start(f32[8,9,8,128]{3,2,1,0:T(8,128)} %shard_map.101), calls=%async_computation.1 | async-start | bytes 589824 | tf_op jit(solution)/shard_map/all_to_all | solution.py:358
  29.8 5.4 %collective-permute-start = (f32[8,8,128]{2,1,0:T(8,128)S(1)}, f32[8,8,128]{2,1,0:T(8,128)S(1)}, u32[]{:S(2)}, u32[]{:S(2)}) collective-permute-start(f32[8,8,128]{2,1,0:T(8,128)S(1)} %get-tuple-element.14), channel_id=1, source_target_pairs={{0,252},{4,0},{8,4},{12,8},{16,12},{20,16},{24,20},{28,24},{32,28}... | collective-permute-start | bytes 98312 | tf_op jit(solution)/shard_map/ppermute | solution.py:362
  35.2 0.1 copy.16
  35.3 0.1 reshape.6.w_feat
  35.5 0.1 copy.20.w_in
  35.6 0.0 copy-start.8
  35.6 0.1 copy.18
  35.7 0.5 copy-done.8
  36.3 0.1 copy.19
  36.4 0.0 copy-start.2
  36.5 0.2 copy.17
  36.7 0.2 collective-permute-done.halo
  36.8 1.8 %all-to-all-done.1.shared = f32[8,9,8,128]{3,2,1,0:T(8,128)S(1)} async-done(((f32[8,9,8,128]{3,2,1,0:T(8,128)}), f32[8,9,8,128]{3,2,1,0:T(8,128)S(1)}, u32[]{:S(2)}, u32[]{:S(2)}) %all-to-all-start.1) | async-done | bytes 294944 | tf_op jit(solution)/shard_map/all_to_all | solution.py:358
  38.7 8.3 %shard_map.102 = (f32[8,9,8,128]{3,2,1,0:T(8,128)S(1)}, f32[8,8,128]{2,1,0:T(8,128)S(1)}, f32[8,8,128]{2,1,0:T(8,128)S(1)}, f32[2,8,128]{2,1,0:T(8,128)S(1)}) custom-call(s32[1]{0:T(128)} %bitcast.me_ref, s32[2]{0:T(128)S(1)} %copy-done.7, s32[2]{0:T(128)S(1)} %copy-done.6, f32[256]{0:T(256)S(1)} %reshape.6.w_feat, f32[4,8,128]{2,1,0:T(8,128)S(1)} %copy-done.5, ...), custom_call_target="tpu_custom_call" | custom-call | tf_op jit(solution)/shard_map/pallas_call | solution.py:343
  47.0 13.2 %all_to_all.26.got = f32[8,9,8,128]{3,2,1,0:T(8,128)S(1)} all-to-all(f32[8,9,8,128]{3,2,1,0:T(8,128)S(1)} %get-tuple-element.16), channel_id=1, replica_groups=mesh['wa_0'=2,'wa_1'=4,'wa_2'=8,'ba'=4] {'wa_2'}, dimensions={0} | all-to-all | bytes 589824 | tf_op jit(solution)/shard_map/all_to_all | solution.py:358
  60.2 0.7 shard_map.103
  60.9 6.7 %all-to-all-start.3 = ((f32[8,9,8,128]{3,2,1,0:T(8,128)}), f32[8,9,8,128]{3,2,1,0:T(8,128)S(1)}, u32[]{:S(2)}, u32[]{:S(2)}) async-start(f32[8,9,8,128]{3,2,1,0:T(8,128)} %shard_map.103), calls=%async_computation.3 | async-start | bytes 589824 | tf_op jit(solution)/shard_map/all_to_all | solution.py:358
  67.7 5.4 %collective-permute-start.2 = (f32[8,8,128]{2,1,0:T(8,128)S(1)}, f32[8,8,128]{2,1,0:T(8,128)S(1)}, u32[]{:S(2)}, u32[]{:S(2)}) collective-permute-start(f32[8,8,128]{2,1,0:T(8,128)S(1)} %get-tuple-element.17.own_in), channel_id=1, source_target_pairs={{0,252},{4,0},{8,4},{12,8},{16,12},{20,16},{24,20},{28,24},{32,28}... | collective-permute-start | bytes 98312 | tf_op jit(solution)/shard_map/ppermute | solution.py:362
  73.1 0.0 collective-permute-start.1
  73.7 0.9 collective-permute-done.2.own_right
  74.7 8.0 %collective-permute-done.1.spill_left = f32[8,8,128]{2,1,0:T(8,128)S(1)} collective-permute-done((f32[8,8,128]{2,1,0:T(8,128)S(1)}, f32[8,8,128]{2,1,0:T(8,128)S(1)}, u32[]{:S(2)}, u32[]{:S(2)}) %collective-permute-start.1) | collective-permute-done | bytes 32800 | tf_op jit(solution)/shard_map/ppermute | solution.py:362
  82.7 8.9 %shard_map.104 = (f32[8,8,128]{2,1,0:T(8,128)S(1)}, f32[8,8,128]{2,1,0:T(8,128)S(1)}, f32[64,1,128]{2,1,0:T(1,128)}) custom-call(s32[2]{0:T(128)S(1)} %copy-done.6, f32[256]{0:T(256)S(1)} %reshape.6.w_feat, f32[1]{0:T(128)S(6)} %copy.22.guidance, f32[2,4,8,128]{3,2,1,0:T(8,128)S(1)} %copy-done.2, f32[8,8,128]{2,1,0:T(8,128)S(1)} %collective-permute-done.halo, ...), custom_call_target="tpu_custom_call" | custom-call | tf_op jit(solution)/shard_map/pallas_call | solution.py:343
  91.6 4.6 %all-to-all-start.4 = ((f32[64,1,128]{2,1,0:T(1,128)}), f32[64,1,128]{2,1,0:T(1,128)S(1)}, u32[]{:S(2)}, u32[]{:S(2)}) async-start(f32[64,1,128]{2,1,0:T(1,128)} %get-tuple-element.20), calls=%async_computation.4 | async-start | bytes 65536 | tf_op jit(solution)/shard_map/all_to_all | solution.py:358
  96.1 1.5 %collective-permute-start.3 = (f32[8,8,128]{2,1,0:T(8,128)S(1)}, f32[8,8,128]{2,1,0:T(8,128)S(1)}, u32[]{:S(2)}, u32[]{:S(2)}) collective-permute-start(f32[8,8,128]{2,1,0:T(8,128)S(1)} %get-tuple-element.22), channel_id=1, source_target_pairs={{0,4},{4,8},{8,12},{12,16},{16,20},{20,24},{24,28},{28,32},{32,36}... | collective-permute-start | bytes 98312 | tf_op jit(solution)/shard_map/ppermute | solution.py:362
  97.7 8.2 %collective-permute-done.3.spill_left = f32[8,8,128]{2,1,0:T(8,128)S(1)} collective-permute-done((f32[8,8,128]{2,1,0:T(8,128)S(1)}, f32[8,8,128]{2,1,0:T(8,128)S(1)}, u32[]{:S(2)}, u32[]{:S(2)}) %collective-permute-start.3) | collective-permute-done | bytes 32800 | tf_op jit(solution)/shard_map/ppermute | solution.py:362
  105.9 2.4 %all-to-all-done.4.squares = f32[64,1,128]{2,1,0:T(1,128)S(1)} async-done(((f32[64,1,128]{2,1,0:T(1,128)}), f32[64,1,128]{2,1,0:T(1,128)S(1)}, u32[]{:S(2)}, u32[]{:S(2)}) %all-to-all-start.4) | async-done | bytes 32800 | tf_op jit(solution)/shard_map/all_to_all | solution.py:358
  108.2 0.8 shard_map.105
  (16 shorter events, 0.0 us)
Async XLA Ops:
  0.0 0.7 copy-start.5
  0.0 0.7 copy-start.6
  0.0 0.7 copy-start.7
  0.7 0.8 copy-start.1
  23.7 11.6 %copy-start.9 = (f32[64,4]{0,1:T(4,128)S(1)}, f32[64,4]{0,1:T(4,128)}, u32[]{:S(2)}) copy-start(f32[64,4]{0,1:T(4,128)} %param.19) | copy-start | bytes 3076
  23.7 11.8 %copy-start.3 = (bf16[320,36]{0,1:T(8,128)(2,1)S(1)}, bf16[320,36]{0,1:T(8,128)(2,1)}, u32[]{:S(2)}) copy-start(bf16[320,36]{0,1:T(8,128)(2,1)} %param.15) | copy-start | bytes 69124
  23.7 11.9 %copy-start.4 = (bf16[36,320]{1,0:T(8,128)(2,1)S(1)}, bf16[36,320]{1,0:T(8,128)(2,1)}, u32[]{:S(2)}) copy-start(bf16[36,320]{1,0:T(8,128)(2,1)} %w_out.3) | copy-start | bytes 69124
  23.7 15.0 %all-to-all-start.1 = ((f32[8,9,8,128]{3,2,1,0:T(8,128)}), f32[8,9,8,128]{3,2,1,0:T(8,128)S(1)}, u32[]{:S(2)}, u32[]{:S(2)}) async-start(f32[8,9,8,128]{3,2,1,0:T(8,128)} %shard_map.101), calls=%async_computation.1 | async-start | bytes 589824 | tf_op jit(solution)/shard_map/all_to_all | solution.py:358
  29.8 6.6 %copy-start = (bf16[320,320]{1,0:T(8,128)(2,1)S(1)}, bf16[320,320]{1,0:T(8,128)(2,1)}, u32[]{:S(2)}) copy-start(bf16[320,320]{1,0:T(8,128)(2,1)} %w_mid.3) | copy-start | bytes 614404
  29.8 7.0 %collective-permute-start = (f32[8,8,128]{2,1,0:T(8,128)S(1)}, f32[8,8,128]{2,1,0:T(8,128)S(1)}, u32[]{:S(2)}, u32[]{:S(2)}) collective-permute-start(f32[8,8,128]{2,1,0:T(8,128)S(1)} %get-tuple-element.14), channel_id=1, source_target_pairs={{0,252},{4,0},{8,4},{12,8},{16,12},{20,16},{24,20},{28,24},{32,28}... | collective-permute-start | bytes 98312 | tf_op jit(solution)/shard_map/ppermute | solution.py:362
  35.6 0.7 copy-start.8
  36.4 2.2 %copy-start.2 = (f32[2,4,8,128]{3,2,1,0:T(8,128)S(1)}, f32[2,4,8,128]{3,2,1,0:T(8,128)}, u32[]{:S(2)}) copy-start(f32[2,4,8,128]{3,2,1,0:T(8,128)} %noise.7) | copy-start | bytes 98308
  60.9 21.8 %all-to-all-start.3 = ((f32[8,9,8,128]{3,2,1,0:T(8,128)}), f32[8,9,8,128]{3,2,1,0:T(8,128)S(1)}, u32[]{:S(2)}, u32[]{:S(2)}) async-start(f32[8,9,8,128]{3,2,1,0:T(8,128)} %shard_map.103), calls=%async_computation.3 | async-start | bytes 589824 | tf_op jit(solution)/shard_map/all_to_all | solution.py:358
  67.7 7.0 %collective-permute-start.2 = (f32[8,8,128]{2,1,0:T(8,128)S(1)}, f32[8,8,128]{2,1,0:T(8,128)S(1)}, u32[]{:S(2)}, u32[]{:S(2)}) collective-permute-start(f32[8,8,128]{2,1,0:T(8,128)S(1)} %get-tuple-element.17.own_in), channel_id=1, source_target_pairs={{0,252},{4,0},{8,4},{12,8},{16,12},{20,16},{24,20},{28,24},{32,28}... | collective-permute-start | bytes 98312 | tf_op jit(solution)/shard_map/ppermute | solution.py:362
  73.1 9.6 %collective-permute-start.1 = (f32[8,8,128]{2,1,0:T(8,128)S(1)}, f32[8,8,128]{2,1,0:T(8,128)S(1)}, u32[]{:S(2)}, u32[]{:S(2)}) collective-permute-start(f32[8,8,128]{2,1,0:T(8,128)S(1)} %get-tuple-element.18.spill_in), channel_id=1, source_target_pairs={{0,4},{4,8},{8,12},{12,16},{16,20},{20,24},{24,28},{28,32},{32,36}... | collective-permute-start | bytes 98312 | tf_op jit(solution)/shard_map/ppermute | solution.py:362
  91.6 16.7 %all-to-all-start.4 = ((f32[64,1,128]{2,1,0:T(1,128)}), f32[64,1,128]{2,1,0:T(1,128)S(1)}, u32[]{:S(2)}, u32[]{:S(2)}) async-start(f32[64,1,128]{2,1,0:T(1,128)} %get-tuple-element.20), calls=%async_computation.4 | async-start | bytes 65536 | tf_op jit(solution)/shard_map/all_to_all | solution.py:358
  96.1 9.7 %collective-permute-start.3 = (f32[8,8,128]{2,1,0:T(8,128)S(1)}, f32[8,8,128]{2,1,0:T(8,128)S(1)}, u32[]{:S(2)}, u32[]{:S(2)}) collective-permute-start(f32[8,8,128]{2,1,0:T(8,128)S(1)} %get-tuple-element.22), channel_id=1, source_target_pairs={{0,4},{4,8},{8,12},{12,16},{16,20},{20,24},{24,28},{28,32},{32,36}... | collective-permute-start | bytes 98312 | tf_op jit(solution)/shard_map/ppermute | solution.py:362

commit v3 on v2

v3 whole, which is shorter than its diff:
```python
import math

import jax
import jax.numpy as jnp
from jax import lax
from jax.experimental import pallas as pl
from jax.experimental.pallas import tpu as pltpu
from jax.sharding import Mesh
from jax.sharding import PartitionSpec as P

C = 4
H = 8
HID = 320
FEAT = 64
WIN = 128
STRIDE = 64
NDEV = 64
NWIN = 128
TAPS = 9 * C
FIELD = H * WIN
OWN = 2
PER_TURN = 16
WA = ("wa_0", "wa_1", "wa_2")
NEAR = "wa_2"
FAR = ("wa_0", "wa_1")
GROUP = 8

TAP_SHIFTS = ((-1, -1), (-1, 0), (-1, 1), (0, -1), (0, 0), (0, 1), (1, -1), (1, 0), (1, 1))
CUMULATIVE_ALPHA = (0.35, 0.55, 0.72, 0.85, 0.93)
STABILITY = 1e-06
ELEMENTS = float(NWIN * C * H * WIN)
F32 = jnp.float32
BF16 = jnp.bfloat16


def plan(number):
    current = CUMULATIVE_ALPHA[number]
    following = CUMULATIVE_ALPHA[number + 1]
    spread = 0.3 * math.sqrt(1.0 - following)
    return (
        math.sqrt(current),
        math.sqrt(1.0 - current),
        math.sqrt(following),
        math.sqrt(1.0 - following - spread * spread),
        spread,
    )


def lanes(shape=(C, H, WIN)):
    return lax.broadcasted_iota(jnp.int32, shape, len(shape) - 1)


def shift_rows(x, by):
    if by == 0:
        return x
    row = lax.broadcasted_iota(jnp.int32, x.shape, 1)
    inside = row >= 1 if by < 0 else row < H - 1
    return jnp.where(inside, pltpu.roll(x, (-by) % H, 1), 0.0)


def shift_lanes(x, by):
    if by == 0:
        return x
    lane = lanes(x.shape)
    inside = lane >= 1 if by < 0 else lane < WIN - 1
    return jnp.where(inside, pltpu.roll(x, (-by) % WIN, 2), 0.0)


def spread_taps(x, sign, tall):
    moved = {by: shift_lanes(x, sign * by) for by in (-1, 0, 1)}
    for k, (down, right) in enumerate(TAP_SHIFTS):
        tall[32 * k : 32 * (k + 1), :] = shift_rows(moved[right], sign * down).reshape(32, WIN)
    rows = [tall[pl.ds(h, TAPS, stride=H), :] for h in range(H)]
    return jnp.concatenate(rows, axis=1).astype(BF16)


def store_taps(tall, values):
    for h in range(H):
        tall[pl.ds(h, TAPS, stride=H), :] = values[:, WIN * h : WIN * (h + 1)]


def gather_taps(tall, sign):
    total = None
    for right in (-1, 0, 1):
        part = None
        for k, (down, across) in enumerate(TAP_SHIFTS):
            if across == right:
                piece = tall[32 * k : 32 * (k + 1), :].reshape(C, H, WIN)
                piece = shift_rows(piece, sign * down)
                part = piece if part is None else part + piece
        part = shift_lanes(part, sign * right)
        total = part if total is None else total + part
    return total


def silu_and_slope(half):
    p = 1.0 + jnp.tanh(half)
    return half * p, p * (1.0 + half * (2.0 - p))


def silu(half):
    return half * (1.0 + jnp.tanh(half))


def dot(a, b):
    return lax.dot_general(a, b, (((1,), (0,)), ((), ())), preferred_element_type=F32)


def predict(windows, weights, embed, talls, slopes):
    shared = range(len(windows))
    halves = [
        (dot(weights["w_in"][...], spread_taps(windows[i], 1, talls[i])) + embed).astype(BF16)
        for i in shared
    ]

    def activated(values, kept, i):
        if i >= OWN:
            return silu(values)
        value, kept[:, i * FIELD : (i + 1) * FIELD] = silu_and_slope(values)
        return value

    middles = [
        dot(weights["w_mid"][...], activated(halves[i], slopes[0], i)).astype(BF16) for i in shared
    ]
    for i in shared:
        joined = (halves[i] + halves[i]) + activated(middles[i], slopes[1], i)
        store_taps(talls[i], dot(weights["w_out"][...], joined))
    return [gather_taps(tall, 1) for tall in talls]


def pull_back(cotangents, weights, talls, slopes):
    own = range(OWN)
    at = [slice(i * FIELD, (i + 1) * FIELD) for i in own]
    d_joined = [
        dot(weights["w_out_t"][...], spread_taps(cotangents[i], -1, talls[i])).astype(BF16)
        for i in own
    ]
    d_active = [
        dot(weights["w_mid_t"][...], d_joined[i] * slopes[1][:, at[i]]).astype(BF16) for i in own
    ]
    for i in own:
        d_hidden = d_joined[i] + d_active[i] * slopes[0][:, at[i]]
        store_taps(talls[i], dot(weights["w_in_t"][...], d_hidden))
    return [gather_taps(tall, -1) for tall in talls]


def percept_pull_back(cleans, anchor, w_feat):
    fields = [[0.5 * x[c] for c in range(C)] for x in (anchor, *cleans)]
    many = len(cleans)

    def some(turn, grads):
        grads = list(grads)
        for i in range(PER_TURN):
            f = turn * PER_TURN + i
            w = [w_feat[f * C + c] for c in range(C)]
            mixed = [(w[0] * x[0] + w[1] * x[1]) + (w[2] * x[2] + w[3] * x[3]) for x in fields]
            target = silu(mixed[0])
            for j in range(many):
                s, slope = silu_and_slope(mixed[1 + j])
                d = (s - target) * slope
                for c in range(C):
                    grads[j * C + c] = grads[j * C + c] + w[c] * d
        return tuple(grads)

    nothing = tuple(jnp.zeros((H, WIN), F32) for _ in range(C * many))
    grads = lax.fori_loop(0, FEAT // PER_TURN, some, nothing)
    return [jnp.stack(grads[C * j : C * (j + 1)]) * (0.5 / FEAT) for j in range(many)]


def cut(first, second, start):
    by = (WIN - start) % WIN
    return jnp.where(
        lanes() < WIN - start, pltpu.roll(first, by, 2), pltpu.roll(second, by, 2)
    )


def place(pieces, starts):
    own, spill = 0.0, 0.0
    for piece, start in zip(pieces, starts):
        moved = pltpu.roll(piece, start, 2)
        inside = lanes() >= start
        own = own + jnp.where(inside, moved, 0.0)
        spill = spill + jnp.where(inside, 0.0, moved)
    return own, spill


def step(number, first, second, starts, anchor, weights, embed_ref, w_feat, scratch):
    now_a, now_s, next_a, direction, _ = plan(number)
    talls, slopes = scratch[:3], scratch[3:5]
    embed = embed_ref[:, number : number + 1]
    windows = [cut(first, second, start) for start in starts]
    every = windows + [anchor]
    predicted = predict(every, weights, embed, talls, slopes)
    cleans = [(w - now_s * p) * (1.0 / now_a) for w, p in zip(every, predicted)]
    d_cleans = percept_pull_back(cleans[:OWN], cleans[OWN], w_feat)
    pulled = pull_back([d * (-now_s / now_a) for d in d_cleans], weights, talls[:OWN], slopes)
    gradients = [d * (1.0 / now_a) + g for d, g in zip(d_cleans, pulled)]
    square = sum(jnp.sum(g * g, axis=0) for g in gradients)
    plain = [
        (next_a / now_a) * (w - now_s * p) + direction * p for w, p in zip(windows, predicted)
    ]
    plain_own, plain_spill = place(plain, starts)
    steep_own, steep_spill = place([g * (-next_a / now_a) for g in gradients], starts)
    return plain_own, plain_spill, steep_own, steep_spill, square


def scale_of(total, guidance):
    return guidance[0] * lax.rsqrt(jnp.full((1, 1, 1), total) * (1.0 / ELEMENTS) + STABILITY)


def opening_kernel(me_ref, offsets, latent, share):
    me = me_ref[0]
    own = latent[...]
    lane = lanes((H, WIN))
    known = jnp.where(
        lane == 2 * me,
        offsets[0].astype(F32),
        jnp.where(lane == 2 * me + 1, offsets[1].astype(F32), 0.0),
    )
    for i in range(GROUP):
        share[i, 0:4] = own
        share[i, 4] = known


def opening_relay_kernel(me_ref, anchors, got, share, beside):
    row, place_in_row = me_ref[0] // GROUP, me_ref[0] % GROUP
    owner = anchors[0] // 2

    def block_of(device):
        return jnp.where(device // GROUP == row, got[device % GROUP, 0:4], 0.0)

    x, y = block_of(owner), block_of((owner + 1) % NDEV)
    right = got[(place_in_row + 1) % GROUP, 0:4]
    known = got[0, 4]
    for i in range(1, GROUP):
        known = known + got[i, 4]
    beside[...] = right
    for i in range(GROUP):
        share[i, 0:4] = x
        share[i, 4:8] = y
        share[i, 8:12] = right
        share[i, 12] = known


def relay_kernel(got, share):
    total = got[0]
    for i in range(1, GROUP):
        total = total + got[i]
    for i in range(GROUP):
        share[i] = total


def weights_of(refs):
    names = ("w_in", "w_mid", "w_out", "w_in_t", "w_mid_t", "w_out_t")
    return dict(zip(names, refs))


def first_kernel(
    me_ref, anchors, offsets, w_feat, latent, noise, beside, shared,
    w_in, w_mid, w_out, w_in_t, w_mid_t, w_out_t, embed,
    share, own_out, spill_out, inverse, *scratch,
):
    weights = weights_of((w_in, w_mid, w_out, w_in_t, w_mid_t, w_out_t))
    me = me_ref[0]

    def summed(at):
        total = shared[0, at]
        for i in range(1, GROUP):
            total = total + shared[i, at]
        return total

    table = summed(12)
    lane = lanes((H, WIN))

    def offset_of(window):
        picked = jnp.where(lane == window, table, 0.0)[0:1]
        return jnp.sum(picked).astype(jnp.int32)

    starts = (offsets[0], STRIDE + offsets[1])
    anchor_at = (anchors[0] % 2) * STRIDE + offset_of(anchors[0])
    anchor = cut(summed(pl.ds(0, 4)), summed(pl.ds(4, 4)), anchor_at)
    across = shared[(me // GROUP + 1) % GROUP, 8:12]
    following = jnp.where(me % GROUP == GROUP - 1, across, beside[...])
    plain_own, plain_spill, steep_own, steep_spill, square = step(
        0, latent[...], following, starts, anchor, weights, embed, w_feat, scratch
    )
    spread = plan(0)[-1]

    def covered(windows):
        count = jnp.zeros((H, WIN), F32)
        for begin in windows:
            count = count + jnp.where((lane >= begin) & (lane < begin + WIN), 1.0, 0.0)
        return 1.0 / count

    left, right = 2 * me + NWIN - 2, 2 * me + 2
    before = (
        offset_of(left % NWIN) - WIN,
        offset_of((left + 1) % NWIN) - STRIDE,
    )
    after = (offset_of(right % NWIN), STRIDE + offset_of((right + 1) % NWIN))
    inverse_own = covered(before + starts)
    inverse_next = covered((starts[0] - WIN, starts[1] - WIN) + after)
    inverse[0] = inverse_own
    inverse[1] = inverse_next
    plain_own = plain_own * inverse_own + spread * noise[0]
    steep_own = steep_own * inverse_own
    plain_spill = plain_spill * inverse_next
    steep_spill = steep_spill * inverse_next
    own_out[0:4] = plain_own
    own_out[4:8] = steep_own
    spill_out[0:4] = plain_spill
    spill_out[4:8] = steep_spill

    owner = anchors[1] // 2
    next_at = (anchors[1] % 2) * STRIDE + offset_of(anchors[1])
    here, ahead, behind = (
        me == owner, me == (owner + 1) % NDEV, me == (owner + NDEV - 1) % NDEV
    )

    def portion(own, spill):
        x = jnp.where(here, own, jnp.where(behind, spill, 0.0))
        y = jnp.where(here, spill, jnp.where(ahead, own, 0.0))
        return cut(x, y, next_at)

    plain_part = portion(plain_own, plain_spill)
    steep_part = portion(steep_own, steep_spill)
    for i in range(GROUP):
        share[i, 0:4] = plain_part
        share[i, 4:8] = steep_part
        share[i, 8] = square


def second_kernel(
    offsets, w_feat, guidance, noise, shared, own_in, spill_in, spill_left, own_right, inverse,
    w_in, w_mid, w_out, w_in_t, w_mid_t, w_out_t, embed,
    own_out, spill_out, square_out, *scratch,
):
    weights = weights_of((w_in, w_mid, w_out, w_in_t, w_mid_t, w_out_t))
    total = shared[0]
    for i in range(1, GROUP):
        total = total + shared[i]
    scale = scale_of(jnp.sum(total[8]), guidance)
    spread = plan(1)[-1]
    anchor = total[0:4] + scale * total[4:8]
    own = own_in[...] + spill_left[...]
    beyond = spill_in[...] + own_right[...]
    first = own[0:4] + scale * own[4:8]
    second = beyond[0:4] + scale * beyond[4:8]
    starts = (offsets[0], STRIDE + offsets[1])
    plain_own, plain_spill, steep_own, steep_spill, square = step(
        1, first, second, starts, anchor, weights, embed, w_feat, scratch
    )
    own_out[0:4] = plain_own * inverse[0] + spread * noise[1]
    own_out[4:8] = steep_own * inverse[0]
    spill_out[0:4] = plain_spill * inverse[1]
    spill_out[4:8] = steep_spill * inverse[1]
    row = jnp.sum(square, axis=0, keepdims=True)
    square_out[...] = jnp.broadcast_to(row[None], (NDEV, 1, WIN))


def closing_kernel(guidance, squares, own_in, spill_left, out):
    scale = scale_of(jnp.sum(squares[...]), guidance)
    own = own_in[...] + spill_left[...]
    out[...] = own[0:4] + scale * own[4:8]


def call(kernel, shapes, n_scalars, *args, scratch=(), megabytes=4):
    in_specs = [
        pl.BlockSpec(memory_space=pltpu.SMEM if i < n_scalars else pltpu.VMEM)
        for i in range(len(args))
    ]
    return pl.pallas_call(
        kernel,
        out_shape=[jax.ShapeDtypeStruct(shape, F32) for shape in shapes],
        in_specs=in_specs,
        out_specs=[pl.BlockSpec(memory_space=pltpu.VMEM) for _ in shapes],
        scratch_shapes=scratch,
        compiler_params=pltpu.CompilerParams(vmem_limit_bytes=megabytes << 20),
    )(*args)


def scratches():
    return (
        [pltpu.VMEM((8 * TAPS, WIN), F32)] * (OWN + 1)
        + [pltpu.VMEM((HID, OWN * FIELD), BF16)] * 2
    )


def exchanged(shares, axes):
    return lax.all_to_all(shares, axes, split_axis=0, concat_axis=0, tiled=True)


def passed_along(shard, by):
    return lax.ppermute(shard, WA, [(i, (i + by) % NDEV) for i in range(NDEV)])


def local(latent, noise, offsets, anchors, guidance, w_in, w_mid, w_out, t_embed, w_feat):
    me = lax.axis_index(WA).astype(jnp.int32).reshape(1)
    features = w_feat.reshape(-1)
    weights = (
        w_in * 0.5, w_mid * 0.5, w_out, w_in.T, w_mid.T * 0.25, w_out.T, t_embed.T * 0.5
    )
    blocks, group = (8, H, WIN), (GROUP, 9, H, WIN)

    (share,) = call(opening_kernel, ((GROUP, 5, H, WIN),), 2, me, offsets, latent)
    share = exchanged(share, NEAR)
    share, beside = call(
        opening_relay_kernel, ((GROUP, 13, H, WIN), (C, H, WIN)), 2, me, anchors, share
    )
    share = exchanged(share, FAR)

    share, own, spill, inverse = call(
        first_kernel, (group, blocks, blocks, (2, H, WIN)), 4,
        me, anchors, offsets, features, latent, noise, beside, share, *weights,
        scratch=scratches(), megabytes=32,
    )
    spill_left = passed_along(spill, 1)
    own_right = passed_along(own, -1)
    share = exchanged(share, NEAR)
    (share,) = call(relay_kernel, (group,), 0, share)
    share = exchanged(share, FAR)

    own, spill, squares = call(
        second_kernel, (blocks, blocks, (NDEV, 1, WIN)), 3,
        offsets, features, guidance, noise, share, own, spill, spill_left, own_right,
        inverse, *weights,
        scratch=scratches(), megabytes=32,
    )
    spill_left = passed_along(spill, 1)
    squares = exchanged(squares, WA)
    (out,) = call(closing_kernel, ((C, H, WIN),), 1, guidance, squares, own, spill_left)
    return out


def solution(mesh):
    finer = Mesh(mesh.devices.reshape(2, 4, 8, mesh.shape["ba"]), ("wa_0", "wa_1", "wa_2", "ba"))
    placed = (P("ba", None, WA), P(None, "ba", None, WA), P(WA), P(), P(), P(), P(), P(), P(), P())
    return jax.shard_map(
        local, mesh=finer, in_specs=placed, out_specs=P("ba", None, WA), check_vma=False
    )
```

time: 110 us -> 99.8 us (0.907)
  blocking collectives: 34 us -> 13.2 us
  starting transfers between devices: 29.9 us -> 38.2 us
  waiting for transfers between devices: 21.6 us -> 28.1 us
  Pallas kernels: 20 us -> 15.5 us
    all_to_all x2 -> x1, blocking collectives: 34 us -> 13.2 us  [exchanged(): return lax.all_to_all(shares, axes, split_axis=0, concat_axis=0, tiled=True)]
    all_to_all x3 -> x4, waiting for transfers between devices: 4.21 us -> 18.8 us  [exchanged(): return lax.all_to_all(shares, axes, split_axis=0, concat_axis=0, tiled=True)]
    all_to_all x3 -> x4, starting transfers between devices: 17.5 us -> 28.8 us  [exchanged(): return lax.all_to_all(shares, axes, split_axis=0, concat_axis=0, tiled=True)]
    ppermute x4 -> x3, waiting for transfers between devices: 17.4 us -> 9.32 us  [passed_along(): return lax.ppermute(shard, WA, [(i, (i + by) % NDEV) for i in range(NDEV)])]
    pallas_call x6, Pallas kernels: 20 us -> 15.5 us  [call(): pl.pallas_call(kernel, out_shape=[jax.ShapeDtypeStruct(shape, F32) for sh...]
    ppermute x4 -> x3, starting transfers between devices: 12.4 us -> 9.41 us  [passed_along(): return lax.ppermute(shard, WA, [(i, (i + by) % NDEV) for i in range(NDEV)])]
    unnamed x25 -> x22, local copies, waits for them, and re-layouts: 2.74 us -> 3.07 us
  transfers between devices with their start and end apart: 7 -> 7, of which waited for: 6 -> 5; matrix products, arithmetic and copies ran while one was open for 1% -> 1% of each run, Pallas kernels for 0% -> 0%
where the time goes in v3:
time: 99.8 us; the launch traced here: 99.1 us
  starting transfers between devices  38.2 us (38%)
  waiting for transfers between devices  28.1 us (28%)
  Pallas kernels  15.5 us (16%)
  blocking collectives  13.2 us (13%)
  local copies, waits for them, and re-layouts  3.31 us (3%)
    all_to_all x4, starting transfers between devices, exchanged(): return lax.all_to_all(shares, axes, split_axis=0, concat_axis=0, tiled=True)  28.8 us
    all_to_all x4, waiting for transfers between devices, exchanged(): return lax.all_to_all(shares, axes, split_axis=0, concat_axis=0, tiled=True)  18.8 us
    pallas_call x6, Pallas kernels, call(): pl.pallas_call(kernel, out_shape=[jax.ShapeDtypeStruct(shape, F32) for sh...  15.5 us
    all_to_all x1, blocking collectives, exchanged(): return lax.all_to_all(shares, axes, split_axis=0, concat_axis=0, tiled=True)  13.2 us
    ppermute x3, starting transfers between devices, passed_along(): return lax.ppermute(shard, WA, [(i, (i + by) % NDEV) for i in range(NDEV)])  9.41 us
    ppermute x3, waiting for transfers between devices, passed_along(): return lax.ppermute(shard, WA, [(i, (i + by) % NDEV) for i in range(NDEV)])  9.32 us
    unnamed x22, local copies, waits for them, and re-layouts  3.07 us
  transfers between devices with their start and end apart: 7, of which 5 were waited for; matrix products, arithmetic and copies ran while one was open for 1% of the time, Pallas kernels for 0%

profile of v3, /device:TPU:2, one launch (start us, length us, event | category | flops | bytes accessed | tf_op | source)
XLA Modules:
  0.0 99.1 jit_solution(7320017243413800692)
XLA Ops:
  0.0 0.7 copy-done.3
  0.7 1.2 %shard_map.100 = f32[8,5,8,128]{3,2,1,0:T(8,128)} custom-call(s32[1]{0:T(128)} %bitcast.me_ref, s32[2]{0:T(128)S(1)} %copy-done.4, f32[4,8,128]{2,1,0:T(8,128)S(1)} %copy-done.3), custom_call_target="tpu_custom_call" | custom-call | tf_op jit(solution)/shard_map/pallas_call | solution.py:372
  1.9 8.6 %all-to-all-start = ((f32[8,5,8,128]{3,2,1,0:T(8,128)}), f32[8,5,8,128]{3,2,1,0:T(8,128)S(1)}, u32[]{:S(2)}, u32[]{:S(2)}) async-start(f32[8,5,8,128]{3,2,1,0:T(8,128)} %shard_map.100), calls=%async_computation | async-start | bytes 327680 | tf_op jit(solution)/shard_map/all_to_all | solution.py:390
  10.6 0.2 copy.24
  10.8 0.0 copy-start
  10.8 0.1 copy.26
  10.9 0.6 copy-done
  11.5 0.1 copy.23
  11.7 0.6 copy-done.1
  12.3 0.1 copy.25
  12.4 0.5 copy-done.8
  13.0 0.1 copy.22
  13.0 0.1 reshape.6.w_feat
  13.2 0.0 copy-start.5
  13.2 7.1 %all-to-all-done.got = f32[8,5,8,128]{3,2,1,0:T(8,128)S(1)} async-done(((f32[8,5,8,128]{3,2,1,0:T(8,128)}), f32[8,5,8,128]{3,2,1,0:T(8,128)S(1)}, u32[]{:S(2)}, u32[]{:S(2)}) %all-to-all-start) | async-done | bytes 163872 | tf_op jit(solution)/shard_map/all_to_all | solution.py:390
  20.3 1.3 %shard_map.101 = (f32[8,13,8,128]{3,2,1,0:T(8,128)}, f32[4,8,128]{2,1,0:T(8,128)S(1)}) custom-call(s32[1]{0:T(128)} %bitcast.me_ref, s32[2]{0:T(128)S(1)} %copy-done.5, f32[8,5,8,128]{3,2,1,0:T(8,128)S(1)} %all-to-all-done.got), custom_call_target="tpu_custom_call" | custom-call | tf_op jit(solution)/shard_map/pallas_call | solution.py:372
  21.7 6.0 %all-to-all-start.1 = ((f32[8,13,8,128]{3,2,1,0:T(8,128)}), f32[8,13,8,128]{3,2,1,0:T(8,128)S(1)}, u32[]{:S(2)}, u32[]{:S(2)}) async-start(f32[8,13,8,128]{3,2,1,0:T(8,128)} %get-tuple-element.15), calls=%async_computation.1 | async-start | bytes 851968 | tf_op jit(solution)/shard_map/all_to_all | solution.py:390
  27.7 0.0 copy-start.2
  27.8 9.3 %all-to-all-done.1.shared = f32[8,13,8,128]{3,2,1,0:T(8,128)S(1)} async-done(((f32[8,13,8,128]{3,2,1,0:T(8,128)}), f32[8,13,8,128]{3,2,1,0:T(8,128)S(1)}, u32[]{:S(2)}, u32[]{:S(2)}) %all-to-all-start.1) | async-done | bytes 426016 | tf_op jit(solution)/shard_map/all_to_all | solution.py:390
  37.1 5.4 %shard_map.102 = (f32[8,9,8,128]{3,2,1,0:T(8,128)S(1)}, f32[8,8,128]{2,1,0:T(8,128)S(1)}, f32[8,8,128]{2,1,0:T(8,128)S(1)}, f32[2,8,128]{2,1,0:T(8,128)S(1)}) custom-call(s32[1]{0:T(128)} %bitcast.me_ref, s32[2]{0:T(128)S(1)} %copy-done.5, s32[2]{0:T(128)S(1)} %copy-done.4, f32[256]{0:T(256)S(1)} %reshape.6.w_feat, f32[4,8,128]{2,1,0:T(8,128)S(1)} %copy-done.3, ...), custom_call_target="tpu_custom_call" | custom-call | tf_op jit(solution)/shard_map/pallas_call | solution.py:372
  42.5 13.2 %all_to_all.25.got = f32[8,9,8,128]{3,2,1,0:T(8,128)S(1)} all-to-all(f32[8,9,8,128]{3,2,1,0:T(8,128)S(1)} %get-tuple-element.16), channel_id=1, replica_groups=mesh['wa_0'=2,'wa_1'=4,'wa_2'=8,'ba'=4] {'wa_2'}, dimensions={0} | all-to-all | bytes 589824 | tf_op jit(solution)/shard_map/all_to_all | solution.py:390
  55.7 0.7 shard_map.103
  56.4 3.5 %all-to-all-start.3 = ((f32[8,9,8,128]{3,2,1,0:T(8,128)}), f32[8,9,8,128]{3,2,1,0:T(8,128)S(1)}, u32[]{:S(2)}, u32[]{:S(2)}) async-start(f32[8,9,8,128]{3,2,1,0:T(8,128)} %shard_map.103), calls=%async_computation.3 | async-start | bytes 589824 | tf_op jit(solution)/shard_map/all_to_all | solution.py:390
  60.0 0.6 collective-permute-start
  60.5 7.2 %collective-permute-start.1 = (f32[8,8,128]{2,1,0:T(8,128)S(1)}, f32[8,8,128]{2,1,0:T(8,128)S(1)}, u32[]{:S(2)}, u32[]{:S(2)}) collective-permute-start(f32[8,8,128]{2,1,0:T(8,128)S(1)} %get-tuple-element.17.own_in), channel_id=1, source_target_pairs={{0,252},{4,0},{8,4},{12,8},{16,12},{20,16},{24,20},{28,24},{32,28}... | collective-permute-start | bytes 98312 | tf_op jit(solution)/shard_map/ppermute | solution.py:394
  68.4 1.2 %collective-permute-done.spill_left = f32[8,8,128]{2,1,0:T(8,128)S(1)} collective-permute-done((f32[8,8,128]{2,1,0:T(8,128)S(1)}, f32[8,8,128]{2,1,0:T(8,128)S(1)}, u32[]{:S(2)}, u32[]{:S(2)}) %collective-permute-start) | collective-permute-done | bytes 32800 | tf_op jit(solution)/shard_map/ppermute | solution.py:394
  69.6 6.0 %shard_map.104 = (f32[8,8,128]{2,1,0:T(8,128)S(1)}, f32[8,8,128]{2,1,0:T(8,128)S(1)}, f32[64,1,128]{2,1,0:T(1,128)}) custom-call(s32[2]{0:T(128)S(1)} %copy-done.4, f32[256]{0:T(256)S(1)} %reshape.6.w_feat, f32[1]{0:T(128)S(6)} %copy.27.guidance, f32[2,4,8,128]{3,2,1,0:T(8,128)S(1)} %copy-done.2, f32[8,9,8,128]{3,2,1,0:T(8,128)S(1)} %all-to-all-done.3.shared, ...), custom_call_target="tpu_custom_call" | custom-call | tf_op jit(solution)/shard_map/pallas_call | solution.py:372
  75.6 10.6 %all-to-all-start.4 = ((f32[64,1,128]{2,1,0:T(1,128)}), f32[64,1,128]{2,1,0:T(1,128)S(1)}, u32[]{:S(2)}, u32[]{:S(2)}) async-start(f32[64,1,128]{2,1,0:T(1,128)} %get-tuple-element.20), calls=%async_computation.4 | async-start | bytes 65536 | tf_op jit(solution)/shard_map/all_to_all | solution.py:390
  86.2 1.6 %collective-permute-start.2 = (f32[8,8,128]{2,1,0:T(8,128)S(1)}, f32[8,8,128]{2,1,0:T(8,128)S(1)}, u32[]{:S(2)}, u32[]{:S(2)}) collective-permute-start(f32[8,8,128]{2,1,0:T(8,128)S(1)} %get-tuple-element.22), channel_id=1, source_target_pairs={{0,4},{4,8},{8,12},{12,16},{16,20},{20,24},{24,28},{28,32},{32,36}... | collective-permute-start | bytes 98312 | tf_op jit(solution)/shard_map/ppermute | solution.py:394
  87.8 8.1 %collective-permute-done.2.spill_left = f32[8,8,128]{2,1,0:T(8,128)S(1)} collective-permute-done((f32[8,8,128]{2,1,0:T(8,128)S(1)}, f32[8,8,128]{2,1,0:T(8,128)S(1)}, u32[]{:S(2)}, u32[]{:S(2)}) %collective-permute-start.2) | collective-permute-done | bytes 32800 | tf_op jit(solution)/shard_map/ppermute | solution.py:394
  95.9 2.4 %all-to-all-done.4.squares = f32[64,1,128]{2,1,0:T(1,128)S(1)} async-done(((f32[64,1,128]{2,1,0:T(1,128)}), f32[64,1,128]{2,1,0:T(1,128)S(1)}, u32[]{:S(2)}, u32[]{:S(2)}) %all-to-all-start.4) | async-done | bytes 32800 | tf_op jit(solution)/shard_map/all_to_all | solution.py:390
  98.3 0.8 shard_map.105
  (17 shorter events, 0.1 us)
Async XLA Ops:
  0.0 0.7 copy-start.3
  0.0 0.7 copy-start.4
  0.7 9.8 %copy-start.6 = (bf16[320,320]{1,0:T(8,128)(2,1)S(1)}, bf16[320,320]{1,0:T(8,128)(2,1)}, u32[]{:S(2)}) copy-start(bf16[320,320]{1,0:T(8,128)(2,1)} %param.16) | copy-start | bytes 614404
  1.9 8.6 %copy-start.7 = (f32[2,320]{1,0:T(2,128)S(1)}, f32[2,320]{1,0:T(2,128)}, u32[]{:S(2)}) copy-start(f32[2,320]{1,0:T(2,128)} %param.18) | copy-start | bytes 7684
  1.9 18.4 %all-to-all-start = ((f32[8,5,8,128]{3,2,1,0:T(8,128)}), f32[8,5,8,128]{3,2,1,0:T(8,128)S(1)}, u32[]{:S(2)}, u32[]{:S(2)}) async-start(f32[8,5,8,128]{3,2,1,0:T(8,128)} %shard_map.100), calls=%async_computation | async-start | bytes 327680 | tf_op jit(solution)/shard_map/all_to_all | solution.py:390
  10.8 0.8 copy-start
  11.5 0.8 copy-start.1
  12.3 0.7 copy-start.8
  13.2 7.2 %copy-start.5 = (s32[2]{0:T(128)S(1)}, s32[2]{0:T(128)}, u32[]{:S(2)}) copy-start(s32[2]{0:T(128)} %anchors.3) | copy-start | bytes 28
  21.7 15.4 %all-to-all-start.1 = ((f32[8,13,8,128]{3,2,1,0:T(8,128)}), f32[8,13,8,128]{3,2,1,0:T(8,128)S(1)}, u32[]{:S(2)}, u32[]{:S(2)}) async-start(f32[8,13,8,128]{3,2,1,0:T(8,128)} %get-tuple-element.15), calls=%async_computation.1 | async-start | bytes 851968 | tf_op jit(solution)/shard_map/all_to_all | solution.py:390
  27.7 9.4 %copy-start.2 = (f32[2,4,8,128]{3,2,1,0:T(8,128)S(1)}, f32[2,4,8,128]{3,2,1,0:T(8,128)}, u32[]{:S(2)}) copy-start(f32[2,4,8,128]{3,2,1,0:T(8,128)} %noise.3) | copy-start | bytes 98308
  56.4 13.2 %all-to-all-start.3 = ((f32[8,9,8,128]{3,2,1,0:T(8,128)}), f32[8,9,8,128]{3,2,1,0:T(8,128)S(1)}, u32[]{:S(2)}, u32[]{:S(2)}) async-start(f32[8,9,8,128]{3,2,1,0:T(8,128)} %shard_map.103), calls=%async_computation.3 | async-start | bytes 589824 | tf_op jit(solution)/shard_map/all_to_all | solution.py:390
  60.0 9.7 %collective-permute-start = (f32[8,8,128]{2,1,0:T(8,128)S(1)}, f32[8,8,128]{2,1,0:T(8,128)S(1)}, u32[]{:S(2)}, u32[]{:S(2)}) collective-permute-start(f32[8,8,128]{2,1,0:T(8,128)S(1)} %get-tuple-element.18.spill_in), channel_id=1, source_target_pairs={{0,4},{4,8},{8,12},{12,16},{16,20},{20,24},{24,28},{28,32},{32,36}... | collective-permute-start | bytes 98312 | tf_op jit(solution)/shard_map/ppermute | solution.py:394
  60.5 9.1 %collective-permute-start.1 = (f32[8,8,128]{2,1,0:T(8,128)S(1)}, f32[8,8,128]{2,1,0:T(8,128)S(1)}, u32[]{:S(2)}, u32[]{:S(2)}) collective-permute-start(f32[8,8,128]{2,1,0:T(8,128)S(1)} %get-tuple-element.17.own_in), channel_id=1, source_target_pairs={{0,252},{4,0},{8,4},{12,8},{16,12},{20,16},{24,20},{28,24},{32,28}... | collective-permute-start | bytes 98312 | tf_op jit(solution)/shard_map/ppermute | solution.py:394
  75.6 22.7 %all-to-all-start.4 = ((f32[64,1,128]{2,1,0:T(1,128)}), f32[64,1,128]{2,1,0:T(1,128)S(1)}, u32[]{:S(2)}, u32[]{:S(2)}) async-start(f32[64,1,128]{2,1,0:T(1,128)} %get-tuple-element.20), calls=%async_computation.4 | async-start | bytes 65536 | tf_op jit(solution)/shard_map/all_to_all | solution.py:390
  86.2 9.7 %collective-permute-start.2 = (f32[8,8,128]{2,1,0:T(8,128)S(1)}, f32[8,8,128]{2,1,0:T(8,128)S(1)}, u32[]{:S(2)}, u32[]{:S(2)}) collective-permute-start(f32[8,8,128]{2,1,0:T(8,128)S(1)} %get-tuple-element.22), channel_id=1, source_target_pairs={{0,4},{4,8},{8,12},{12,16},{16,20},{20,24},{24,28},{28,32},{32,36}... | collective-permute-start | bytes 98312 | tf_op jit(solution)/shard_map/ppermute | solution.py:394

commit v4 on v3

--- a/solution.py
+++ b/solution.py
@@ -152,7 +152,7 @@
         grads = list(grads)
         for i in range(PER_TURN):
             f = turn * PER_TURN + i
-            w = [w_feat[f * C + c] for c in range(C)]
+            w = [w_feat[c, f] for c in range(C)]
             mixed = [(w[0] * x[0] + w[1] * x[1]) + (w[2] * x[2] + w[3] * x[3]) for x in fields]
             target = silu(mixed[0])
             for j in range(many):
@@ -168,7 +168,7 @@
 
 
 def cut(first, second, start):
-    by = (WIN - start) % WIN
+    by = (WIN - start) & (WIN - 1)
     return jnp.where(
         lanes() < WIN - start, pltpu.roll(first, by, 2), pltpu.roll(second, by, 2)
     )
@@ -187,12 +187,14 @@
 def step(number, first, second, starts, anchor, weights, embed_ref, w_feat, scratch):
     now_a, now_s, next_a, direction, _ = plan(number)
     talls, slopes = scratch[:3], scratch[3:5]
-    embed = embed_ref[:, number : number + 1]
+    embed = jnp.concatenate([embed_ref[number]] * (FIELD // WIN), axis=1)
     windows = [cut(first, second, start) for start in starts]
     every = windows + [anchor]
     predicted = predict(every, weights, embed, talls, slopes)
     cleans = [(w - now_s * p) * (1.0 / now_a) for w, p in zip(every, predicted)]
-    d_cleans = percept_pull_back(cleans[:OWN], cleans[OWN], w_feat)
+    feat_copy, feat_held = w_feat
+    feat_copy.wait()
+    d_cleans = percept_pull_back(cleans[:OWN], cleans[OWN], feat_held)
     pulled = pull_back([d * (-now_s / now_a) for d in d_cleans], weights, talls[:OWN], slopes)
     gradients = [d * (1.0 / now_a) + g for d, g in zip(d_cleans, pulled)]
     square = sum(jnp.sum(g * g, axis=0) for g in gradients)
@@ -205,35 +207,45 @@
 
 
 def scale_of(total, guidance):
-    return guidance[0] * lax.rsqrt(jnp.full((1, 1, 1), total) * (1.0 / ELEMENTS) + STABILITY)
-
-
-def opening_kernel(me_ref, offsets, latent, share):
-    me = me_ref[0]
-    own = latent[...]
+    return guidance[...] * lax.rsqrt(jnp.full((H, WIN), total) * (1.0 / ELEMENTS) + STABILITY)
+
+
+def opening_kernel(
+    guidance, offsets, latent, t_embed, share, strength, t_embed_held, held, shifts, arrived
+):
+    copies = [
+        pltpu.make_async_copy(latent, held, arrived.at[0]),
+        pltpu.make_async_copy(offsets, shifts, arrived.at[1]),
+        pltpu.make_async_copy(t_embed, t_embed_held, arrived.at[2]),
+    ]
+    for copy in copies:
+        copy.start()
+    strength[...] = jnp.full((H, WIN), guidance[0])
+    for copy in copies:
+        copy.wait()
+    own = held[...]
     lane = lanes((H, WIN))
     known = jnp.where(
-        lane == 2 * me,
-        offsets[0].astype(F32),
-        jnp.where(lane == 2 * me + 1, offsets[1].astype(F32), 0.0),
+        lane == 0, shifts[0].astype(F32), jnp.where(lane == 1, shifts[1].astype(F32), 0.0)
     )
     for i in range(GROUP):
         share[i, 0:4] = own
         share[i, 4] = known
 
 
-def opening_relay_kernel(me_ref, anchors, got, share, beside):
-    row, place_in_row = me_ref[0] // GROUP, me_ref[0] % GROUP
-    owner = anchors[0] // 2
+def opening_relay_kernel(anchors, got, share, beside):
+    row, column = lax.axis_index(FAR), lax.axis_index(NEAR)
+    owner = anchors[0] >> 1
 
     def block_of(device):
-        return jnp.where(device // GROUP == row, got[device % GROUP, 0:4], 0.0)
-
-    x, y = block_of(owner), block_of((owner + 1) % NDEV)
-    right = got[(place_in_row + 1) % GROUP, 0:4]
+        return jnp.where(device >> 3 == row, got[device & 7, 0:4], 0.0)
+
+    x, y = block_of(owner), block_of((owner + 1) & (NDEV - 1))
+    right = got[(column + 1) & 7, 0:4]
     known = got[0, 4]
     for i in range(1, GROUP):
-        known = known + got[i, 4]
+        known = known + pltpu.roll(got[i, 4], 2 * i, 1)
+    known = pltpu.roll(known, 2 * GROUP * row, 1)
     beside[...] = right
     for i in range(GROUP):
         share[i, 0:4] = x
@@ -250,18 +262,45 @@
         share[i] = total
 
 
+def prepare(w_in_t, w_mid, w_out, t_embed, w_in, w_mid_half, w_mid_t, w_out_t, embed):
+    def turned(values, factor):
+        return (values.astype(F32).T * factor).astype(BF16)
+
+    w_in[...] = turned(w_in_t[...], 0.5)
+    w_mid_half[...] = (w_mid[...].astype(F32) * 0.5).astype(BF16)
+    w_mid_t[...] = turned(w_mid[...], 0.25)
+    w_out_t[...] = turned(w_out[...], 1.0)
+    for number in range(2):
+        row = jnp.broadcast_to(t_embed[number : number + 1, :] * 0.5, (WIN, HID))
+        embed[number] = row.T
+
+
+def fetches(noise, w_feat, scratch):
+    noise_held, feat_held, arrived = scratch[:3]
+    noise_copy = pltpu.make_async_copy(noise, noise_held, arrived.at[0])
+    feat_copy = pltpu.make_async_copy(w_feat, feat_held, arrived.at[1])
+    noise_copy.start()
+    feat_copy.start()
+    return noise_copy, feat_copy, noise_held, feat_held, scratch[3:]
+
+
+def offset_in(table, window):
+    row = table[0:1, :]
+    return jnp.sum(jnp.where(lanes((1, WIN)) == window, row, 0.0)).astype(jnp.int32)
+
+
 def weights_of(refs):
     names = ("w_in", "w_mid", "w_out", "w_in_t", "w_mid_t", "w_out_t")
     return dict(zip(names, refs))
 
 
 def first_kernel(
-    me_ref, anchors, offsets, w_feat, latent, noise, beside, shared,
-    w_in, w_mid, w_out, w_in_t, w_mid_t, w_out_t, embed,
-    share, own_out, spill_out, inverse, *scratch,
+    anchors, w_feat, noise, latent, beside, shared,
+    w_in_t, w_mid, w_out, t_embed,
+    share, own_out, spill_out, inverse, table_out, w_in, w_mid_half, w_mid_t, w_out_t, embed,
+    *scratch,
 ):
-    weights = weights_of((w_in, w_mid, w_out, w_in_t, w_mid_t, w_out_t))
-    me = me_ref[0]
+    table_held, table_arrived, *scratch = scratch
 
     def summed(at):
         total = shared[0, at]
@@ -269,20 +308,26 @@
             total = total + shared[i, at]
         return total
 
-    table = summed(12)
+    table_out[...] = summed(12)
+    table_copy = pltpu.make_async_copy(table_out, table_held, table_arrived)
+    table_copy.start()
+    noise_copy, feat_copy, noise_held, feat_held, scratch = fetches(noise.at[0], w_feat, scratch)
+    prepare(w_in_t, w_mid, w_out, t_embed, w_in, w_mid_half, w_mid_t, w_out_t, embed)
+    weights = weights_of((w_in, w_mid_half, w_out, w_in_t, w_mid_t, w_out_t))
+    me = lax.axis_index(WA)
     lane = lanes((H, WIN))
+    table_copy.wait()
 
     def offset_of(window):
-        picked = jnp.where(lane == window, table, 0.0)[0:1]
-        return jnp.sum(picked).astype(jnp.int32)
-
-    starts = (offsets[0], STRIDE + offsets[1])
-    anchor_at = (anchors[0] % 2) * STRIDE + offset_of(anchors[0])
+        return table_held[0, window].astype(jnp.int32)
+
+    starts = (offset_of(2 * me), STRIDE + offset_of(2 * me + 1))
+    anchor_at = (anchors[0] & 1) * STRIDE + offset_of(anchors[0])
     anchor = cut(summed(pl.ds(0, 4)), summed(pl.ds(4, 4)), anchor_at)
-    across = shared[(me // GROUP + 1) % GROUP, 8:12]
-    following = jnp.where(me % GROUP == GROUP - 1, across, beside[...])
+    across = shared[((me >> 3) + 1) & 7, 8:12]
+    following = jnp.where(me & 7 == 7, across, beside[...])
     plain_own, plain_spill, steep_own, steep_spill, square = step(
-        0, latent[...], following, starts, anchor, weights, embed, w_feat, scratch
+        0, latent[...], following, starts, anchor, weights, embed, (feat_copy, feat_held), scratch
     )
     spread = plan(0)[-1]
 
@@ -294,15 +339,16 @@
 
     left, right = 2 * me + NWIN - 2, 2 * me + 2
     before = (
-        offset_of(left % NWIN) - WIN,
-        offset_of((left + 1) % NWIN) - STRIDE,
-    )
-    after = (offset_of(right % NWIN), STRIDE + offset_of((right + 1) % NWIN))
+        offset_of(left & (NWIN - 1)) - WIN,
+        offset_of((left + 1) & (NWIN - 1)) - STRIDE,
+    )
+    after = (offset_of(right & (NWIN - 1)), STRIDE + offset_of((right + 1) & (NWIN - 1)))
     inverse_own = covered(before + starts)
     inverse_next = covered((starts[0] - WIN, starts[1] - WIN) + after)
     inverse[0] = inverse_own
     inverse[1] = inverse_next
-    plain_own = plain_own * inverse_own + spread * noise[0]
+    noise_copy.wait()
+    plain_own = plain_own * inverse_own + spread * noise_held[...]
     steep_own = steep_own * inverse_own
     plain_spill = plain_spill * inverse_next
     steep_spill = steep_spill * inverse_next
@@ -311,10 +357,10 @@
     spill_out[0:4] = plain_spill
     spill_out[4:8] = steep_spill
 
-    owner = anchors[1] // 2
-    next_at = (anchors[1] % 2) * STRIDE + offset_of(anchors[1])
+    owner = anchors[1] >> 1
+    next_at = (anchors[1] & 1) * STRIDE + offset_of(anchors[1])
     here, ahead, behind = (
-        me == owner, me == (owner + 1) % NDEV, me == (owner + NDEV - 1) % NDEV
+        me == owner, me == (owner + 1) & (NDEV - 1), me == (owner - 1) & (NDEV - 1)
     )
 
     def portion(own, spill):
@@ -331,10 +377,13 @@
 
 
 def second_kernel(
-    offsets, w_feat, guidance, noise, shared, own_in, spill_in, spill_left, own_right, inverse,
+    w_feat, noise, guidance, table, shared, own_in, spill_in, spill_left, own_right, inverse,
     w_in, w_mid, w_out, w_in_t, w_mid_t, w_out_t, embed,
     own_out, spill_out, square_out, *scratch,
 ):
+    noise_copy, feat_copy, noise_held, feat_held, scratch = fetches(noise.at[1], w_feat, scratch)
+    me = lax.axis_index(WA)
+    starts = (offset_in(table, 2 * me), STRIDE + offset_in(table, 2 * me + 1))
     weights = weights_of((w_in, w_mid, w_out, w_in_t, w_mid_t, w_out_t))
     total = shared[0]
     for i in range(1, GROUP):
@@ -346,11 +395,11 @@
     beyond = spill_in[...] + own_right[...]
     first = own[0:4] + scale * own[4:8]
     second = beyond[0:4] + scale * beyond[4:8]
-    starts = (offsets[0], STRIDE + offsets[1])
     plain_own, plain_spill, steep_own, steep_spill, square = step(
-        1, first, second, starts, anchor, weights, embed, w_feat, scratch
-    )
-    own_out[0:4] = plain_own * inverse[0] + spread * noise[1]
+        1, first, second, starts, anchor, weights, embed, (feat_copy, feat_held), scratch
+    )
+    noise_copy.wait()
+    own_out[0:4] = plain_own * inverse[0] + spread * noise_held[...]
     own_out[4:8] = steep_own * inverse[0]
     spill_out[0:4] = plain_spill * inverse[1]
     spill_out[4:8] = steep_spill * inverse[1]
@@ -364,14 +413,23 @@
     out[...] = own[0:4] + scale * own[4:8]
 
 
-def call(kernel, shapes, n_scalars, *args, scratch=(), megabytes=4):
+def call(kernel, shapes, spaces, *args, scratch=(), megabytes=4, near=True):
+    kinds = {"s": pltpu.SMEM, "h": pltpu.HBM, "v": pltpu.VMEM}
     in_specs = [
-        pl.BlockSpec(memory_space=pltpu.SMEM if i < n_scalars else pltpu.VMEM)
-        for i in range(len(args))
+        pl.BlockSpec(memory_space=kinds[letter]) for letter in spaces.ljust(len(args), "v")
+    ]
+    args = [
+        pltpu.with_memory_space_constraint(arg, pltpu.HBM) if letter == "h" else arg
+        for arg, letter in zip(args, spaces.ljust(len(args), "v"))
     ]
     return pl.pallas_call(
         kernel,
-        out_shape=[jax.ShapeDtypeStruct(shape, F32) for shape in shapes],
+        out_shape=[
+            (pltpu.VMEM if near else jax.ShapeDtypeStruct)(
+                *(shape if isinstance(shape[0], tuple) else (shape, F32))
+            )
+            for shape in shapes
+        ],
         in_specs=in_specs,
         out_specs=[pl.BlockSpec(memory_space=pltpu.VMEM) for _ in shapes],
         scratch_shapes=scratch,
@@ -390,45 +448,62 @@
     return lax.all_to_all(shares, axes, split_axis=0, concat_axis=0, tiled=True)
 
 
-def passed_along(shard, by):
-    return lax.ppermute(shard, WA, [(i, (i + by) % NDEV) for i in range(NDEV)])
+def passed_along(shard, axes, by):
+    length = lax.axis_size(axes)
+    return lax.ppermute(shard, axes, [(i, (i + by) % length) for i in range(length)])
 
 
 def local(latent, noise, offsets, anchors, guidance, w_in, w_mid, w_out, t_embed, w_feat):
-    me = lax.axis_index(WA).astype(jnp.int32).reshape(1)
-    features = w_feat.reshape(-1)
-    weights = (
-        w_in * 0.5, w_mid * 0.5, w_out, w_in.T, w_mid.T * 0.25, w_out.T, t_embed.T * 0.5
-    )
-    blocks, group = (8, H, WIN), (GROUP, 9, H, WIN)
-
-    (share,) = call(opening_kernel, ((GROUP, 5, H, WIN),), 2, me, offsets, latent)
+    features = w_feat.T
+    blocks = (8, H, WIN)
+    tall, square = ((HID, TAPS), BF16), ((HID, HID), BF16)
+    noise_place = [
+        pltpu.VMEM((C, H, WIN), F32), pltpu.SMEM((C, FEAT), F32), pltpu.SemaphoreType.DMA((2,))
+    ]
+
+    share, strength, t_embed = call(
+        opening_kernel, ((GROUP, 5, H, WIN), (H, WIN), (2, HID)), "shhh",
+        guidance, offsets, latent, t_embed,
+        scratch=[
+            pltpu.VMEM((C, H, WIN), F32), pltpu.SMEM((2,), jnp.int32),
+            pltpu.SemaphoreType.DMA((3,)),
+        ],
+    )
     share = exchanged(share, NEAR)
     share, beside = call(
-        opening_relay_kernel, ((GROUP, 13, H, WIN), (C, H, WIN)), 2, me, anchors, share
+        opening_relay_kernel, ((GROUP, 13, H, WIN), (C, H, WIN)), "s", anchors, share
     )
     share = exchanged(share, FAR)
 
-    share, own, spill, inverse = call(
-        first_kernel, (group, blocks, blocks, (2, H, WIN)), 4,
-        me, anchors, offsets, features, latent, noise, beside, share, *weights,
-        scratch=scratches(), megabytes=32,
-    )
-    spill_left = passed_along(spill, 1)
-    own_right = passed_along(own, -1)
+    share, own, spill, inverse, table, w_in_half, w_mid_half, w_mid_t, w_out_t, embed = call(
+        first_kernel,
+        (
+            (GROUP, 9, H, WIN), blocks, blocks, (2, H, WIN), (H, WIN),
+            tall, square, square, tall, (2, HID, WIN),
+        ),
+        "shh",
+        anchors, features, noise, latent, beside, share,
+        w_in.T, w_mid, w_out, t_embed,
+        scratch=[pltpu.SMEM((H, WIN), F32), pltpu.SemaphoreType.DMA] + noise_place + scratches(),
+        megabytes=32,
+    )
+    spill_left = passed_along(spill, WA, 1)
+    own_right = passed_along(own, WA, -1)
     share = exchanged(share, NEAR)
-    (share,) = call(relay_kernel, (group,), 0, share)
+    (share,) = call(relay_kernel, ((GROUP, 9, H, WIN),), "", share)
     share = exchanged(share, FAR)
 
     own, spill, squares = call(
-        second_kernel, (blocks, blocks, (NDEV, 1, WIN)), 3,
-        offsets, features, guidance, noise, share, own, spill, spill_left, own_right,
-        inverse, *weights,
-        scratch=scratches(), megabytes=32,
-    )
-    spill_left = passed_along(spill, 1)
+        second_kernel, (blocks, blocks, (NDEV, 1, WIN)), "hh",
+        features, noise, strength, table, share, own, spill, spill_left, own_right,
+        inverse, w_in_half, w_mid_half, w_out, w_in.T, w_mid_t, w_out_t, embed,
+        scratch=noise_place + scratches(), megabytes=32,
+    )
+    spill_left = passed_along(spill, WA, 1)
     squares = exchanged(squares, WA)
-    (out,) = call(closing_kernel, ((C, H, WIN),), 1, guidance, squares, own, spill_left)
+    (out,) = call(
+        closing_kernel, ((C, H, WIN),), "", strength, squares, own, spill_left, near=False
+    )
     return out
 
 

time: 99.8 us -> 97.9 us (0.981)
  blocking collectives: 13.2 us -> 46.9 us
  starting transfers between devices: 38.2 us -> 14.9 us
  waiting for transfers between devices: 28.1 us -> 20.2 us
  local copies, waits for them, and re-layouts: 3.31 us -> 0.02 us
    all_to_all x1 -> x3, blocking collectives: 13.2 us -> 46.9 us  [exchanged(): return lax.all_to_all(shares, axes, split_axis=0, concat_axis=0, tiled=True)]
    all_to_all x4 -> x2, starting transfers between devices: 28.8 us -> 8.03 us  [exchanged(): return lax.all_to_all(shares, axes, split_axis=0, concat_axis=0, tiled=True)]
    all_to_all x4 -> x2, waiting for transfers between devices: 18.8 us -> 2.37 us  [exchanged(): return lax.all_to_all(shares, axes, split_axis=0, concat_axis=0, tiled=True)]
    ppermute x3, waiting for transfers between devices: 9.32 us -> 17.8 us  [passed_along(): lax.ppermute(shard, axes, [(i, (i + by) % length) for i in range(length)])]
    unnamed x22 -> x10, local copies, waits for them, and re-layouts: 3.07 us -> 0.02 us
    ppermute x3, starting transfers between devices: 9.41 us -> 6.89 us  [passed_along(): lax.ppermute(shard, axes, [(i, (i + by) % length) for i in range(length)])]
  transfers between devices with their start and end apart: 7 -> 5, of which waited for: 5 -> 4; matrix products, arithmetic and copies ran while one was open for 1% -> 0% of each run, Pallas kernels for 0% -> 0%
where the time goes in v4:
time: 97.9 us; the launch traced here: 97.5 us
  blocking collectives  46.9 us (48%)
  waiting for transfers between devices  20.2 us (21%)
  starting transfers between devices  14.9 us (15%)
  Pallas kernels  14.8 us (15%)
    all_to_all x3, blocking collectives, exchanged(): return lax.all_to_all(shares, axes, split_axis=0, concat_axis=0, tiled=True)  46.9 us
    ppermute x3, waiting for transfers between devices, passed_along(): lax.ppermute(shard, axes, [(i, (i + by) % length) for i in range(length)])  17.8 us
    pallas_call x6, Pallas kernels, call(): pl.pallas_call(kernel, out_shape=[(pltpu.VMEM if near else jax.ShapeDtype...  14.8 us
    all_to_all x2, starting transfers between devices, exchanged(): return lax.all_to_all(shares, axes, split_axis=0, concat_axis=0, tiled=True)  8.03 us
    ppermute x3, starting transfers between devices, passed_along(): lax.ppermute(shard, axes, [(i, (i + by) % length) for i in range(length)])  6.89 us
    all_to_all x2, waiting for transfers between devices, exchanged(): return lax.all_to_all(shares, axes, split_axis=0, concat_axis=0, tiled=True)  2.37 us
  transfers between devices with their start and end apart: 5, of which 4 were waited for; matrix products, arithmetic and copies ran while one was open for 0% of the time, Pallas kernels for 0%

profile of v4, /device:TPU:2, one launch (start us, length us, event | category | flops | bytes accessed | tf_op | source)
XLA Modules:
  0.0 97.5 jit_solution(14858036972486070612)
XLA Ops:
  0.7 0.8 shard_map.100
  1.5 0.0 copy-start.4
  1.5 18.0 %all_to_all.25.got = f32[8,5,8,128]{3,2,1,0:T(8,128)S(1)} all-to-all(f32[8,5,8,128]{3,2,1,0:T(8,128)S(1)} %get-tuple-element.24), channel_id=1, replica_groups=mesh['wa_0'=2,'wa_1'=4,'wa_2'=8,'ba'=4] {'wa_2'}, dimensions={0} | all-to-all | bytes 327680 | tf_op jit(solution)/shard_map/all_to_all | solution.py:448
  19.5 0.0 copy-done.4
  19.5 0.7 shard_map.101
  20.2 0.0 copy-start
  20.2 0.0 copy-start.1
  20.2 0.0 copy-start.2
  20.2 0.0 copy-start.3
  20.2 15.6 %all_to_all.26.shared = f32[8,13,8,128]{3,2,1,0:T(8,128)S(1)} all-to-all(f32[8,13,8,128]{3,2,1,0:T(8,128)S(1)} %get-tuple-element.26), channel_id=1, replica_groups=mesh['wa_0'=2,'wa_1'=4,'wa_2'=8,'ba'=4] {'wa_0','wa_1'}, dimensions={0} | all-to-all | bytes 851968 | tf_op jit(solution)/shard_map/all_to_all | solution.py:448
  35.9 0.0 copy-done
  35.9 0.0 copy-done.1
  35.9 0.0 copy-done.2
  35.9 0.0 copy-done.3
  35.9 6.2 %shard_map.102 = (f32[8,9,8,128]{3,2,1,0:T(8,128)S(1)}, f32[8,8,128]{2,1,0:T(8,128)S(1)}, f32[8,8,128]{2,1,0:T(8,128)S(1)}, f32[2,8,128]{2,1,0:T(8,128)S(1)}, f3...) custom-call(s32[2]{0:T(128)S(1)} %copy-done.4, ...), custom_call_target="tpu_custom_call" | custom-call | tf_op jit(solution)/shard_map/pallas_call | solution.py:425
  42.1 13.2 %all_to_all.27.got = f32[8,9,8,128]{3,2,1,0:T(8,128)S(1)} all-to-all(f32[8,9,8,128]{3,2,1,0:T(8,128)S(1)} %get-tuple-element.29), channel_id=1, replica_groups=mesh['wa_0'=2,'wa_1'=4,'wa_2'=8,'ba'=4] {'wa_2'}, dimensions={0} | all-to-all | bytes 589824 | tf_op jit(solution)/shard_map/all_to_all | solution.py:448
  55.3 0.7 shard_map.103
  56.0 3.4 %all-to-all-start.3 = ((f32[8,9,8,128]{3,2,1,0:T(8,128)}), f32[8,9,8,128]{3,2,1,0:T(8,128)S(1)}, u32[]{:S(2)}, u32[]{:S(2)}) async-start(f32[8,9,8,128]{3,2,1,0:T(8,128)} %shard_map.103), calls=%async_computation.3 | async-start | bytes 589824 | tf_op jit(solution)/shard_map/all_to_all | solution.py:448
  59.5 5.4 %collective-permute-start.1 = (f32[8,8,128]{2,1,0:T(8,128)S(1)}, f32[8,8,128]{2,1,0:T(8,128)S(1)}, u32[]{:S(2)}, u32[]{:S(2)}) collective-permute-start(f32[8,8,128]{2,1,0:T(8,128)S(1)} %get-tuple-element.30.own_in), channel_id=1, source_target_pairs={{0,252},{4,0},{8,4},{12,8},{16,12},{20,16},{24,20},{28,24},{32,28}... | collective-permute-start | bytes 98312 | tf_op jit(solution)/shard_map/ppermute | solution.py:453
  64.8 0.0 collective-permute-start
  64.8 1.6 %collective-permute-done.1.own_right = f32[8,8,128]{2,1,0:T(8,128)S(1)} collective-permute-done((f32[8,8,128]{2,1,0:T(8,128)S(1)}, f32[8,8,128]{2,1,0:T(8,128)S(1)}, u32[]{:S(2)}, u32[]{:S(2)}) %collective-permute-start.1) | collective-permute-done | bytes 32800 | tf_op jit(solution)/shard_map/ppermute | solution.py:453
  66.4 8.0 %collective-permute-done.spill_left = f32[8,8,128]{2,1,0:T(8,128)S(1)} collective-permute-done((f32[8,8,128]{2,1,0:T(8,128)S(1)}, f32[8,8,128]{2,1,0:T(8,128)S(1)}, u32[]{:S(2)}, u32[]{:S(2)}) %collective-permute-start) | collective-permute-done | bytes 32800 | tf_op jit(solution)/shard_map/ppermute | solution.py:453
  74.5 0.0 all-to-all-done.3.shared
  74.5 5.5 %shard_map.104 = (f32[8,8,128]{2,1,0:T(8,128)S(1)}, f32[8,8,128]{2,1,0:T(8,128)S(1)}, f32[64,1,128]{2,1,0:T(1,128)}) custom-call(f32[4,64]{1,0:T(4,128)} %bitcast.5, f32[2,4,8,128]{3,2,1,0:T(8,128)} %noise.3, f32[8,128]{1,0:T(8,128)S(1)} %get-tuple-element.23.guidance, f32[8,128]{1,0:T(8,128)S(1)} %get-tuple-element.28.table, ...), custom_call_target="tpu_custom_call" | custom-call | tf_op jit(solution)/shard_map/pallas_call | solution.py:425
  80.0 4.6 %all-to-all-start.4 = ((f32[64,1,128]{2,1,0:T(1,128)}), f32[64,1,128]{2,1,0:T(1,128)S(1)}, u32[]{:S(2)}, u32[]{:S(2)}) async-start(f32[64,1,128]{2,1,0:T(1,128)} %get-tuple-element.38), calls=%async_computation.4 | async-start | bytes 65536 | tf_op jit(solution)/shard_map/all_to_all | solution.py:448
  84.6 1.5 %collective-permute-start.2 = (f32[8,8,128]{2,1,0:T(8,128)S(1)}, f32[8,8,128]{2,1,0:T(8,128)S(1)}, u32[]{:S(2)}, u32[]{:S(2)}) collective-permute-start(f32[8,8,128]{2,1,0:T(8,128)S(1)} %get-tuple-element.40), channel_id=1, source_target_pairs={{0,4},{4,8},{8,12},{12,16},{16,20},{20,24},{24,28},{28,32},{32,36}... | collective-permute-start | bytes 98312 | tf_op jit(solution)/shard_map/ppermute | solution.py:453
  86.2 8.2 %collective-permute-done.2.spill_left = f32[8,8,128]{2,1,0:T(8,128)S(1)} collective-permute-done((f32[8,8,128]{2,1,0:T(8,128)S(1)}, f32[8,8,128]{2,1,0:T(8,128)S(1)}, u32[]{:S(2)}, u32[]{:S(2)}) %collective-permute-start.2) | collective-permute-done | bytes 32800 | tf_op jit(solution)/shard_map/ppermute | solution.py:453
  94.3 2.4 %all-to-all-done.4.squares = f32[64,1,128]{2,1,0:T(1,128)S(1)} async-done(((f32[64,1,128]{2,1,0:T(1,128)}), f32[64,1,128]{2,1,0:T(1,128)S(1)}, u32[]{:S(2)}, u32[]{:S(2)}) %all-to-all-start.4) | async-done | bytes 32800 | tf_op jit(solution)/shard_map/all_to_all | solution.py:448
  96.7 0.8 shard_map.105
Async XLA Ops:
  1.5 18.0 %copy-start.4 = (s32[2]{0:T(128)S(1)}, s32[2]{0:T(128)}, u32[]{:S(2)}) copy-start(s32[2]{0:T(128)} %anchors.3) | copy-start | bytes 28
  20.2 15.6 %copy-start = (bf16[320,320]{1,0:T(8,128)(2,1)S(1)}, bf16[320,320]{1,0:T(8,128)(2,1)}, u32[]{:S(2)}) copy-start(bf16[320,320]{1,0:T(8,128)(2,1)} %w_mid.1) | copy-start | bytes 614404
  20.2 15.6 %copy-start.1 = (bf16[320,36]{0,1:T(8,128)(2,1)S(1)}, bf16[320,36]{0,1:T(8,128)(2,1)}, u32[]{:S(2)}) copy-start(bf16[320,36]{0,1:T(8,128)(2,1)} %param.15) | copy-start | bytes 69124
  20.2 15.6 %copy-start.2 = (bf16[36,320]{1,0:T(8,128)(2,1)S(1)}, bf16[36,320]{1,0:T(8,128)(2,1)}, u32[]{:S(2)}) copy-start(bf16[36,320]{1,0:T(8,128)(2,1)} %w_out.3) | copy-start | bytes 69124
  20.2 15.6 %copy-start.3 = (f32[4,8,128]{2,1,0:T(8,128)S(1)}, f32[4,8,128]{2,1,0:T(8,128)}, u32[]{:S(2)}) copy-start(f32[4,8,128]{2,1,0:T(8,128)} %latent.3) | copy-start | bytes 49156
  56.0 18.4 %all-to-all-start.3 = ((f32[8,9,8,128]{3,2,1,0:T(8,128)}), f32[8,9,8,128]{3,2,1,0:T(8,128)S(1)}, u32[]{:S(2)}, u32[]{:S(2)}) async-start(f32[8,9,8,128]{3,2,1,0:T(8,128)} %shard_map.103), calls=%async_computation.3 | async-start | bytes 589824 | tf_op jit(solution)/shard_map/all_to_all | solution.py:448
  59.5 7.0 %collective-permute-start.1 = (f32[8,8,128]{2,1,0:T(8,128)S(1)}, f32[8,8,128]{2,1,0:T(8,128)S(1)}, u32[]{:S(2)}, u32[]{:S(2)}) collective-permute-start(f32[8,8,128]{2,1,0:T(8,128)S(1)} %get-tuple-element.30.own_in), channel_id=1, source_target_pairs={{0,252},{4,0},{8,4},{12,8},{16,12},{20,16},{24,20},{28,24},{32,28}... | collective-permute-start | bytes 98312 | tf_op jit(solution)/shard_map/ppermute | solution.py:453
  64.8 9.6 %collective-permute-start = (f32[8,8,128]{2,1,0:T(8,128)S(1)}, f32[8,8,128]{2,1,0:T(8,128)S(1)}, u32[]{:S(2)}, u32[]{:S(2)}) collective-permute-start(f32[8,8,128]{2,1,0:T(8,128)S(1)} %get-tuple-element.31.spill_in), channel_id=1, source_target_pairs={{0,4},{4,8},{8,12},{12,16},{16,20},{20,24},{24,28},{28,32},{32,36}... | collective-permute-start | bytes 98312 | tf_op jit(solution)/shard_map/ppermute | solution.py:453
  80.0 16.7 %all-to-all-start.4 = ((f32[64,1,128]{2,1,0:T(1,128)}), f32[64,1,128]{2,1,0:T(1,128)S(1)}, u32[]{:S(2)}, u32[]{:S(2)}) async-start(f32[64,1,128]{2,1,0:T(1,128)} %get-tuple-element.38), calls=%async_computation.4 | async-start | bytes 65536 | tf_op jit(solution)/shard_map/all_to_all | solution.py:448
  84.6 9.7 %collective-permute-start.2 = (f32[8,8,128]{2,1,0:T(8,128)S(1)}, f32[8,8,128]{2,1,0:T(8,128)S(1)}, u32[]{:S(2)}, u32[]{:S(2)}) collective-permute-start(f32[8,8,128]{2,1,0:T(8,128)S(1)} %get-tuple-element.40), channel_id=1, source_target_pairs={{0,4},{4,8},{8,12},{12,16},{16,20},{20,24},{24,28},{28,32},{32,36}... | collective-permute-start | bytes 98312 | tf_op jit(solution)/shard_map/ppermute | solution.py:453

commit v5 on v4

--- a/solution.py
+++ b/solution.py
@@ -184,7 +184,9 @@
     return own, spill
 
 
-def step(number, first, second, starts, anchor, weights, embed_ref, w_feat, scratch):
+def step(
+    number, first, second, starts, anchor, weights, embed_ref, w_feat, scratch, prepare=lambda: None
+):
     now_a, now_s, next_a, direction, _ = plan(number)
     talls, slopes = scratch[:3], scratch[3:5]
     embed = jnp.concatenate([embed_ref[number]] * (FIELD // WIN), axis=1)
@@ -192,6 +194,7 @@
     every = windows + [anchor]
     predicted = predict(every, weights, embed, talls, slopes)
     cleans = [(w - now_s * p) * (1.0 / now_a) for w, p in zip(every, predicted)]
+    prepare()
     feat_copy, feat_held = w_feat
     feat_copy.wait()
     d_cleans = percept_pull_back(cleans[:OWN], cleans[OWN], feat_held)
@@ -262,17 +265,12 @@
         share[i] = total
 
 
-def prepare(w_in_t, w_mid, w_out, t_embed, w_in, w_mid_half, w_mid_t, w_out_t, embed):
-    def turned(values, factor):
-        return (values.astype(F32).T * factor).astype(BF16)
-
-    w_in[...] = turned(w_in_t[...], 0.5)
-    w_mid_half[...] = (w_mid[...].astype(F32) * 0.5).astype(BF16)
-    w_mid_t[...] = turned(w_mid[...], 0.25)
-    w_out_t[...] = turned(w_out[...], 1.0)
-    for number in range(2):
-        row = jnp.broadcast_to(t_embed[number : number + 1, :] * 0.5, (WIN, HID))
-        embed[number] = row.T
+def turned(values, factor):
+    return (values.astype(F32).T * factor).astype(BF16)
+
+
+def column_of(row):
+    return jnp.broadcast_to(row * 0.5, (WIN, HID)).T
 
 
 def fetches(noise, w_feat, scratch):
@@ -297,7 +295,7 @@
 def first_kernel(
     anchors, w_feat, noise, latent, beside, shared,
     w_in_t, w_mid, w_out, t_embed,
-    share, own_out, spill_out, inverse, table_out, w_in, w_mid_half, w_mid_t, w_out_t, embed,
+    share, own_out, spill_out, inside, outside, inverse, table_out, w_in, w_mid_half, w_mid_t, w_out_t, embed,
     *scratch,
 ):
     table_held, table_arrived, *scratch = scratch
@@ -312,7 +310,15 @@
     table_copy = pltpu.make_async_copy(table_out, table_held, table_arrived)
     table_copy.start()
     noise_copy, feat_copy, noise_held, feat_held, scratch = fetches(noise.at[0], w_feat, scratch)
-    prepare(w_in_t, w_mid, w_out, t_embed, w_in, w_mid_half, w_mid_t, w_out_t, embed)
+    w_in[...] = turned(w_in_t[...], 0.5)
+    w_mid_half[...] = (w_mid[...].astype(F32) * 0.5).astype(BF16)
+    embed[0] = column_of(t_embed[0:1, :])
+
+    def prepare():
+        w_mid_t[...] = turned(w_mid[...], 0.25)
+        w_out_t[...] = turned(w_out[...], 1.0)
+        embed[1] = column_of(t_embed[1:2, :])
+
     weights = weights_of((w_in, w_mid_half, w_out, w_in_t, w_mid_t, w_out_t))
     me = lax.axis_index(WA)
     lane = lanes((H, WIN))
@@ -327,7 +333,8 @@
     across = shared[((me >> 3) + 1) & 7, 8:12]
     following = jnp.where(me & 7 == 7, across, beside[...])
     plain_own, plain_spill, steep_own, steep_spill, square = step(
-        0, latent[...], following, starts, anchor, weights, embed, (feat_copy, feat_held), scratch
+        0, latent[...], following, starts, anchor, weights, embed, (feat_copy, feat_held), scratch,
+        prepare,
     )
     spread = plan(0)[-1]
 
@@ -356,6 +363,10 @@
     own_out[4:8] = steep_own
     spill_out[0:4] = plain_spill
     spill_out[4:8] = steep_spill
+    odd = me & 1 == 1
+    for at, own, spill in ((0, plain_own, plain_spill), (4, steep_own, steep_spill)):
+        inside[at : at + 4] = jnp.where(odd, own, spill)
+        outside[at : at + 4] = jnp.where(odd, spill, own)
 
     owner = anchors[1] >> 1
     next_at = (anchors[1] & 1) * STRIDE + offset_of(anchors[1])
@@ -377,7 +388,7 @@
 
 
 def second_kernel(
-    w_feat, noise, guidance, table, shared, own_in, spill_in, spill_left, own_right, inverse,
+    w_feat, noise, guidance, table, shared, own_in, spill_in, inside, outside, inverse,
     w_in, w_mid, w_out, w_in_t, w_mid_t, w_out_t, embed,
     own_out, spill_out, square_out, *scratch,
 ):
@@ -391,8 +402,9 @@
     scale = scale_of(jnp.sum(total[8]), guidance)
     spread = plan(1)[-1]
     anchor = total[0:4] + scale * total[4:8]
-    own = own_in[...] + spill_left[...]
-    beyond = spill_in[...] + own_right[...]
+    odd = me & 1 == 1
+    own = own_in[...] + jnp.where(odd, inside[...], outside[...])
+    beyond = spill_in[...] + jnp.where(odd, outside[...], inside[...])
     first = own[0:4] + scale * own[4:8]
     second = beyond[0:4] + scale * beyond[4:8]
     plain_own, plain_spill, steep_own, steep_spill, square = step(
@@ -453,6 +465,11 @@
     return lax.ppermute(shard, axes, [(i, (i + by) % length) for i in range(length)])
 
 
+def swapped(shard, first):
+    pairs = [((first + i) % NDEV, (first + (i ^ 1)) % NDEV) for i in range(NDEV)]
+    return lax.ppermute(shard, WA, pairs)
+
+
 def local(latent, noise, offsets, anchors, guidance, w_in, w_mid, w_out, t_embed, w_feat):
     features = w_feat.T
     blocks = (8, H, WIN)
@@ -475,10 +492,10 @@
     )
     share = exchanged(share, FAR)
 
-    share, own, spill, inverse, table, w_in_half, w_mid_half, w_mid_t, w_out_t, embed = call(
+    share, own, spill, inside, outside, inverse, table, w_in_half, w_mid_half, w_mid_t, w_out_t, embed = call(
         first_kernel,
         (
-            (GROUP, 9, H, WIN), blocks, blocks, (2, H, WIN), (H, WIN),
+            (GROUP, 9, H, WIN), blocks, blocks, blocks, blocks, (2, H, WIN), (H, WIN),
             tall, square, square, tall, (2, HID, WIN),
         ),
         "shh",
@@ -487,15 +504,15 @@
         scratch=[pltpu.SMEM((H, WIN), F32), pltpu.SemaphoreType.DMA] + noise_place + scratches(),
         megabytes=32,
     )
-    spill_left = passed_along(spill, WA, 1)
-    own_right = passed_along(own, WA, -1)
+    inside = swapped(inside, 0)
+    outside = swapped(outside, 1)
     share = exchanged(share, NEAR)
     (share,) = call(relay_kernel, ((GROUP, 9, H, WIN),), "", share)
     share = exchanged(share, FAR)
 
     own, spill, squares = call(
         second_kernel, (blocks, blocks, (NDEV, 1, WIN)), "hh",
-        features, noise, strength, table, share, own, spill, spill_left, own_right,
+        features, noise, strength, table, share, own, spill, inside, outside,
         inverse, w_in_half, w_mid_half, w_out, w_in.T, w_mid_t, w_out_t, embed,
         scratch=noise_place + scratches(), megabytes=32,
     )

time: 97.9 us -> 96.2 us (0.983)
  waiting for transfers between devices: 20.2 us -> 14.6 us
  starting transfers between devices: 14.9 us -> 18.9 us
    ppermute x3 -> x1, waiting for transfers between devices: 17.8 us -> 8.08 us  [passed_along(): lax.ppermute(shard, axes, [(i, (i + by) % length) for i in range(length)])]
    ppermute x0 -> x2, starting transfers between devices: none -> 6.05 us  [swapped(): return lax.ppermute(shard, WA, pairs)]
    ppermute x3 -> x1, starting transfers between devices: 6.89 us -> 1.65 us  [passed_along(): lax.ppermute(shard, axes, [(i, (i + by) % length) for i in range(length)])]
    ppermute x0 -> x2, waiting for transfers between devices: none -> 4.2 us  [swapped(): return lax.ppermute(shard, WA, pairs)]
    all_to_all x2, starting transfers between devices: 8.03 us -> 11.2 us  [exchanged(): return lax.all_to_all(shares, axes, split_axis=0, concat_axis=0, tiled=True)]
  transfers between devices with their start and end apart: 5 -> 5, of which waited for: 4 -> 3; matrix products, arithmetic and copies ran while one was open for 0% -> 0% of each run, Pallas kernels for 0% -> 0%
where the time goes in v5:
time: 96.2 us; the launch traced here: 95.8 us
  blocking collectives  46.9 us (49%)
  starting transfers between devices  18.9 us (20%)
  Pallas kernels  14.7 us (15%)
  waiting for transfers between devices  14.6 us (15%)
    all_to_all x3, blocking collectives, exchanged(): return lax.all_to_all(shares, axes, split_axis=0, concat_axis=0, tiled=True)  46.9 us
    pallas_call x6, Pallas kernels, call(): pl.pallas_call(kernel, out_shape=[(pltpu.VMEM if near else jax.ShapeDtype...  14.7 us
    all_to_all x2, starting transfers between devices, exchanged(): return lax.all_to_all(shares, axes, split_axis=0, concat_axis=0, tiled=True)  11.2 us
    ppermute x1, waiting for transfers between devices, passed_along(): lax.ppermute(shard, axes, [(i, (i + by) % length) for i in range(length)])  8.08 us
    ppermute x2, starting transfers between devices, swapped(): return lax.ppermute(shard, WA, pairs)  6.05 us
    ppermute x2, waiting for transfers between devices, swapped(): return lax.ppermute(shard, WA, pairs)  4.2 us
    all_to_all x2, waiting for transfers between devices, exchanged(): return lax.all_to_all(shares, axes, split_axis=0, concat_axis=0, tiled=True)  2.37 us
  transfers between devices with their start and end apart: 5, of which 3 were waited for; matrix products, arithmetic and copies ran while one was open for 0% of the time, Pallas kernels for 0%

profile of v5, /device:TPU:2, one launch (start us, length us, event | category | flops | bytes accessed | tf_op | source)
XLA Modules:
  0.0 95.8 jit_solution(12031637394705937112)
XLA Ops:
  0.7 0.8 shard_map.100
  1.5 0.0 copy-start.4
  1.5 18.0 %all_to_all.25.got = f32[8,5,8,128]{3,2,1,0:T(8,128)S(1)} all-to-all(f32[8,5,8,128]{3,2,1,0:T(8,128)S(1)} %get-tuple-element.26), channel_id=1, replica_groups=mesh['wa_0'=2,'wa_1'=4,'wa_2'=8,'ba'=4] {'wa_2'}, dimensions={0} | all-to-all | bytes 327680 | tf_op jit(solution)/shard_map/all_to_all | solution.py:460
  19.5 0.0 copy-done.4
  19.5 0.7 shard_map.101
  20.2 0.0 copy-start
  20.2 0.0 copy-start.1
  20.2 0.0 copy-start.2
  20.2 0.0 copy-start.3
  20.2 15.6 %all_to_all.26.shared = f32[8,13,8,128]{3,2,1,0:T(8,128)S(1)} all-to-all(f32[8,13,8,128]{3,2,1,0:T(8,128)S(1)} %get-tuple-element.28), channel_id=1, replica_groups=mesh['wa_0'=2,'wa_1'=4,'wa_2'=8,'ba'=4] {'wa_0','wa_1'}, dimensions={0} | all-to-all | bytes 851968 | tf_op jit(solution)/shard_map/all_to_all | solution.py:460
  35.9 0.0 copy-done
  35.9 0.0 copy-done.1
  35.9 0.0 copy-done.2
  35.9 0.0 copy-done.3
  35.9 6.2 %shard_map.102 = (f32[8,9,8,128]{3,2,1,0:T(8,128)S(1)}, f32[8,8,128]{2,1,0:T(8,128)S(1)}, f32[8,8,128]{2,1,0:T(8,128)S(1)}, f32[8,8,128]{2,1,0:T(8,128)S(1)}, f3...) custom-call(s32[2]{0:T(128)S(1)} %copy-done.4, ...), custom_call_target="tpu_custom_call" | custom-call | tf_op jit(solution)/shard_map/pallas_call | solution.py:437
  42.1 13.2 %all_to_all.27.got = f32[8,9,8,128]{3,2,1,0:T(8,128)S(1)} all-to-all(f32[8,9,8,128]{3,2,1,0:T(8,128)S(1)} %get-tuple-element.31), channel_id=1, replica_groups=mesh['wa_0'=2,'wa_1'=4,'wa_2'=8,'ba'=4] {'wa_2'}, dimensions={0} | all-to-all | bytes 589824 | tf_op jit(solution)/shard_map/all_to_all | solution.py:460
  55.3 0.7 shard_map.103
  56.0 3.4 %all-to-all-start.3 = ((f32[8,9,8,128]{3,2,1,0:T(8,128)}), f32[8,9,8,128]{3,2,1,0:T(8,128)S(1)}, u32[]{:S(2)}, u32[]{:S(2)}) async-start(f32[8,9,8,128]{3,2,1,0:T(8,128)} %shard_map.103), calls=%async_computation.3 | async-start | bytes 589824 | tf_op jit(solution)/shard_map/all_to_all | solution.py:460
  59.4 0.6 collective-permute-start
  60.0 5.4 %collective-permute-start.1 = (f32[8,8,128]{2,1,0:T(8,128)S(1)}, f32[8,8,128]{2,1,0:T(8,128)S(1)}, u32[]{:S(2)}, u32[]{:S(2)}) collective-permute-start(f32[8,8,128]{2,1,0:T(8,128)S(1)} %get-tuple-element.35), channel_id=1, source_target_pairs={{4,8},{8,4},{12,16},{16,12},{20,24},{24,20},{28,32},{32,28},{36,40... | collective-permute-start | bytes 98312 | tf_op jit(solution)/shard_map/ppermute | solution.py:470
  65.5 0.0 collective-permute-done.inside
  65.5 4.2 %collective-permute-done.1.outside = f32[8,8,128]{2,1,0:T(8,128)S(1)} collective-permute-done((f32[8,8,128]{2,1,0:T(8,128)S(1)}, f32[8,8,128]{2,1,0:T(8,128)S(1)}, u32[]{:S(2)}, u32[]{:S(2)}) %collective-permute-start.1) | collective-permute-done | bytes 32800 | tf_op jit(solution)/shard_map/ppermute | solution.py:470
  69.7 0.0 all-to-all-done.3.shared
  69.7 5.5 %shard_map.104 = (f32[8,8,128]{2,1,0:T(8,128)S(1)}, f32[8,8,128]{2,1,0:T(8,128)S(1)}, f32[64,1,128]{2,1,0:T(1,128)}) custom-call(f32[4,64]{1,0:T(4,128)} %bitcast.5, f32[2,4,8,128]{3,2,1,0:T(8,128)} %noise.3, f32[8,128]{1,0:T(8,128)S(1)} %get-tuple-element.25.guidance, f32[8,128]{1,0:T(8,128)S(1)} %get-tuple-element.30.table, ...), custom_call_target="tpu_custom_call" | custom-call | tf_op jit(solution)/shard_map/pallas_call | solution.py:437
  75.2 7.7 %all-to-all-start.4 = ((f32[64,1,128]{2,1,0:T(1,128)}), f32[64,1,128]{2,1,0:T(1,128)S(1)}, u32[]{:S(2)}, u32[]{:S(2)}) async-start(f32[64,1,128]{2,1,0:T(1,128)} %get-tuple-element.42), calls=%async_computation.4 | async-start | bytes 65536 | tf_op jit(solution)/shard_map/all_to_all | solution.py:460
  82.9 1.6 %collective-permute-start.2 = (f32[8,8,128]{2,1,0:T(8,128)S(1)}, f32[8,8,128]{2,1,0:T(8,128)S(1)}, u32[]{:S(2)}, u32[]{:S(2)}) collective-permute-start(f32[8,8,128]{2,1,0:T(8,128)S(1)} %get-tuple-element.44), channel_id=1, source_target_pairs={{0,4},{4,8},{8,12},{12,16},{16,20},{20,24},{24,28},{28,32},{32,36}... | collective-permute-start | bytes 98312 | tf_op jit(solution)/shard_map/ppermute | solution.py:465
  84.6 8.1 %collective-permute-done.2.spill_left = f32[8,8,128]{2,1,0:T(8,128)S(1)} collective-permute-done((f32[8,8,128]{2,1,0:T(8,128)S(1)}, f32[8,8,128]{2,1,0:T(8,128)S(1)}, u32[]{:S(2)}, u32[]{:S(2)}) %collective-permute-start.2) | collective-permute-done | bytes 32800 | tf_op jit(solution)/shard_map/ppermute | solution.py:465
  92.7 2.4 %all-to-all-done.4.squares = f32[64,1,128]{2,1,0:T(1,128)S(1)} async-done(((f32[64,1,128]{2,1,0:T(1,128)}), f32[64,1,128]{2,1,0:T(1,128)S(1)}, u32[]{:S(2)}, u32[]{:S(2)}) %all-to-all-start.4) | async-done | bytes 32800 | tf_op jit(solution)/shard_map/all_to_all | solution.py:460
  95.0 0.8 shard_map.105
Async XLA Ops:
  1.5 18.0 %copy-start.4 = (s32[2]{0:T(128)S(1)}, s32[2]{0:T(128)}, u32[]{:S(2)}) copy-start(s32[2]{0:T(128)} %anchors.3) | copy-start | bytes 28
  20.2 15.6 %copy-start = (bf16[320,320]{1,0:T(8,128)(2,1)S(1)}, bf16[320,320]{1,0:T(8,128)(2,1)}, u32[]{:S(2)}) copy-start(bf16[320,320]{1,0:T(8,128)(2,1)} %w_mid.1) | copy-start | bytes 614404
  20.2 15.6 %copy-start.1 = (bf16[320,36]{0,1:T(8,128)(2,1)S(1)}, bf16[320,36]{0,1:T(8,128)(2,1)}, u32[]{:S(2)}) copy-start(bf16[320,36]{0,1:T(8,128)(2,1)} %param.15) | copy-start | bytes 69124
  20.2 15.6 %copy-start.2 = (bf16[36,320]{1,0:T(8,128)(2,1)S(1)}, bf16[36,320]{1,0:T(8,128)(2,1)}, u32[]{:S(2)}) copy-start(bf16[36,320]{1,0:T(8,128)(2,1)} %w_out.3) | copy-start | bytes 69124
  20.2 15.6 %copy-start.3 = (f32[4,8,128]{2,1,0:T(8,128)S(1)}, f32[4,8,128]{2,1,0:T(8,128)}, u32[]{:S(2)}) copy-start(f32[4,8,128]{2,1,0:T(8,128)} %latent.3) | copy-start | bytes 49156
  56.0 13.7 %all-to-all-start.3 = ((f32[8,9,8,128]{3,2,1,0:T(8,128)}), f32[8,9,8,128]{3,2,1,0:T(8,128)S(1)}, u32[]{:S(2)}, u32[]{:S(2)}) async-start(f32[8,9,8,128]{3,2,1,0:T(8,128)} %shard_map.103), calls=%async_computation.3 | async-start | bytes 589824 | tf_op jit(solution)/shard_map/all_to_all | solution.py:460
  59.4 6.1 %collective-permute-start = (f32[8,8,128]{2,1,0:T(8,128)S(1)}, f32[8,8,128]{2,1,0:T(8,128)S(1)}, u32[]{:S(2)}, u32[]{:S(2)}) collective-permute-start(f32[8,8,128]{2,1,0:T(8,128)S(1)} %get-tuple-element.34), channel_id=1, source_target_pairs={{0,4},{4,0},{8,12},{12,8},{16,20},{20,16},{24,28},{28,24},{32,36},... | collective-permute-start | bytes 98312 | tf_op jit(solution)/shard_map/ppermute | solution.py:470
  60.0 9.6 %collective-permute-start.1 = (f32[8,8,128]{2,1,0:T(8,128)S(1)}, f32[8,8,128]{2,1,0:T(8,128)S(1)}, u32[]{:S(2)}, u32[]{:S(2)}) collective-permute-start(f32[8,8,128]{2,1,0:T(8,128)S(1)} %get-tuple-element.35), channel_id=1, source_target_pairs={{4,8},{8,4},{12,16},{16,12},{20,24},{24,20},{28,32},{32,28},{36,40... | collective-permute-start | bytes 98312 | tf_op jit(solution)/shard_map/ppermute | solution.py:470
  75.2 19.8 %all-to-all-start.4 = ((f32[64,1,128]{2,1,0:T(1,128)}), f32[64,1,128]{2,1,0:T(1,128)S(1)}, u32[]{:S(2)}, u32[]{:S(2)}) async-start(f32[64,1,128]{2,1,0:T(1,128)} %get-tuple-element.42), calls=%async_computation.4 | async-start | bytes 65536 | tf_op jit(solution)/shard_map/all_to_all | solution.py:460
  82.9 9.7 %collective-permute-start.2 = (f32[8,8,128]{2,1,0:T(8,128)S(1)}, f32[8,8,128]{2,1,0:T(8,128)S(1)}, u32[]{:S(2)}, u32[]{:S(2)}) collective-permute-start(f32[8,8,128]{2,1,0:T(8,128)S(1)} %get-tuple-element.44), channel_id=1, source_target_pairs={{0,4},{4,8},{8,12},{12,16},{16,20},{20,24},{24,28},{28,32},{32,36}... | collective-permute-start | bytes 98312 | tf_op jit(solution)/shard_map/ppermute | solution.py:465

commit v6 on v5

--- a/solution.py
+++ b/solution.py
@@ -295,10 +295,12 @@
 def first_kernel(
     anchors, w_feat, noise, latent, beside, shared,
     w_in_t, w_mid, w_out, t_embed,
-    share, own_out, spill_out, inside, outside, inverse, table_out, w_in, w_mid_half, w_mid_t, w_out_t, embed,
-    *scratch,
+    share, own_out, spill_out, inside, outside, inverse, table_out,
+    w_in, w_mid_half, w_mid_t, w_out_t, embed, *scratch,
 ):
     table_held, table_arrived, *scratch = scratch
+    table_copy = pltpu.make_async_copy(shared.at[:, 12, 0:1], table_held, table_arrived)
+    table_copy.start()
 
     def summed(at):
         total = shared[0, at]
@@ -307,8 +309,6 @@
         return total
 
     table_out[...] = summed(12)
-    table_copy = pltpu.make_async_copy(table_out, table_held, table_arrived)
-    table_copy.start()
     noise_copy, feat_copy, noise_held, feat_held, scratch = fetches(noise.at[0], w_feat, scratch)
     w_in[...] = turned(w_in_t[...], 0.5)
     w_mid_half[...] = (w_mid[...].astype(F32) * 0.5).astype(BF16)
@@ -325,7 +325,7 @@
     table_copy.wait()
 
     def offset_of(window):
-        return table_held[0, window].astype(jnp.int32)
+        return table_held[window >> 4, 0, window].astype(jnp.int32)
 
     starts = (offset_of(2 * me), STRIDE + offset_of(2 * me + 1))
     anchor_at = (anchors[0] & 1) * STRIDE + offset_of(anchors[0])
@@ -501,11 +501,13 @@
         "shh",
         anchors, features, noise, latent, beside, share,
         w_in.T, w_mid, w_out, t_embed,
-        scratch=[pltpu.SMEM((H, WIN), F32), pltpu.SemaphoreType.DMA] + noise_place + scratches(),
+        scratch=[pltpu.SMEM((GROUP, 1, WIN), F32), pltpu.SemaphoreType.DMA]
+        + noise_place
+        + scratches(),
         megabytes=32,
     )
+    outside = swapped(outside, 1)
     inside = swapped(inside, 0)
-    outside = swapped(outside, 1)
     share = exchanged(share, NEAR)
     (share,) = call(relay_kernel, ((GROUP, 9, H, WIN),), "", share)
     share = exchanged(share, FAR)

time: 96.2 us -> 96.2 us (level)
  no operation moved by 1% of the time
where the time goes in v6:
time: 96.2 us; the launch traced here: 95.8 us
  blocking collectives  46.9 us (49%)
  starting transfers between devices  18.9 us (20%)
  Pallas kernels  14.7 us (15%)
  waiting for transfers between devices  14.6 us (15%)
    all_to_all x3, blocking collectives, exchanged(): return lax.all_to_all(shares, axes, split_axis=0, concat_axis=0, tiled=True)  46.9 us
    pallas_call x6, Pallas kernels, call(): pl.pallas_call(kernel, out_shape=[(pltpu.VMEM if near else jax.ShapeDtype...  14.7 us
    all_to_all x2, starting transfers between devices, exchanged(): return lax.all_to_all(shares, axes, split_axis=0, concat_axis=0, tiled=True)  11.2 us
    ppermute x1, waiting for transfers between devices, passed_along(): lax.ppermute(shard, axes, [(i, (i + by) % length) for i in range(length)])  8.08 us
    ppermute x2, starting transfers between devices, swapped(): return lax.ppermute(shard, WA, pairs)  6.05 us
    ppermute x2, waiting for transfers between devices, swapped(): return lax.ppermute(shard, WA, pairs)  4.2 us
    all_to_all x2, waiting for transfers between devices, exchanged(): return lax.all_to_all(shares, axes, split_axis=0, concat_axis=0, tiled=True)  2.37 us
  transfers between devices with their start and end apart: 5, of which 3 were waited for; matrix products, arithmetic and copies ran while one was open for 0% of the time, Pallas kernels for 0%

profile of v6, /device:TPU:2, one launch (start us, length us, event | category | flops | bytes accessed | tf_op | source)
XLA Modules:
  0.0 95.8 jit_solution(3494843125501151693)
XLA Ops:
  0.7 0.8 shard_map.100
  1.5 0.0 copy-start.4
  1.5 18.0 %all_to_all.25.got = f32[8,5,8,128]{3,2,1,0:T(8,128)S(1)} all-to-all(f32[8,5,8,128]{3,2,1,0:T(8,128)S(1)} %get-tuple-element.26), channel_id=1, replica_groups=mesh['wa_0'=2,'wa_1'=4,'wa_2'=8,'ba'=4] {'wa_2'}, dimensions={0} | all-to-all | bytes 327680 | tf_op jit(solution)/shard_map/all_to_all | solution.py:460
  19.5 0.0 copy-done.4
  19.5 0.7 shard_map.101
  20.2 0.0 copy-start
  20.2 0.0 copy-start.1
  20.2 0.0 copy-start.2
  20.2 0.0 copy-start.3
  20.2 15.6 %all_to_all.26.shared = f32[8,13,8,128]{3,2,1,0:T(8,128)S(1)} all-to-all(f32[8,13,8,128]{3,2,1,0:T(8,128)S(1)} %get-tuple-element.28), channel_id=1, replica_groups=mesh['wa_0'=2,'wa_1'=4,'wa_2'=8,'ba'=4] {'wa_0','wa_1'}, dimensions={0} | all-to-all | bytes 851968 | tf_op jit(solution)/shard_map/all_to_all | solution.py:460
  35.9 0.0 copy-done
  35.9 0.0 copy-done.1
  35.9 0.0 copy-done.2
  35.9 0.0 copy-done.3
  35.9 6.1 %shard_map.102 = (f32[8,9,8,128]{3,2,1,0:T(8,128)S(1)}, f32[8,8,128]{2,1,0:T(8,128)S(1)}, f32[8,8,128]{2,1,0:T(8,128)S(1)}, f32[8,8,128]{2,1,0:T(8,128)S(1)}, f3...) custom-call(s32[2]{0:T(128)S(1)} %copy-done.4, ...), custom_call_target="tpu_custom_call" | custom-call | tf_op jit(solution)/shard_map/pallas_call | solution.py:437
  42.0 13.2 %all_to_all.27.got = f32[8,9,8,128]{3,2,1,0:T(8,128)S(1)} all-to-all(f32[8,9,8,128]{3,2,1,0:T(8,128)S(1)} %get-tuple-element.31), channel_id=1, replica_groups=mesh['wa_0'=2,'wa_1'=4,'wa_2'=8,'ba'=4] {'wa_2'}, dimensions={0} | all-to-all | bytes 589824 | tf_op jit(solution)/shard_map/all_to_all | solution.py:460
  55.2 0.7 shard_map.103
  55.9 3.4 %all-to-all-start.3 = ((f32[8,9,8,128]{3,2,1,0:T(8,128)}), f32[8,9,8,128]{3,2,1,0:T(8,128)S(1)}, u32[]{:S(2)}, u32[]{:S(2)}) async-start(f32[8,9,8,128]{3,2,1,0:T(8,128)} %shard_map.103), calls=%async_computation.3 | async-start | bytes 589824 | tf_op jit(solution)/shard_map/all_to_all | solution.py:460
  59.4 0.6 collective-permute-start
  60.0 5.4 %collective-permute-start.1 = (f32[8,8,128]{2,1,0:T(8,128)S(1)}, f32[8,8,128]{2,1,0:T(8,128)S(1)}, u32[]{:S(2)}, u32[]{:S(2)}) collective-permute-start(f32[8,8,128]{2,1,0:T(8,128)S(1)} %get-tuple-element.35), channel_id=1, source_target_pairs={{4,8},{8,4},{12,16},{16,12},{20,24},{24,20},{28,32},{32,28},{36,40... | collective-permute-start | bytes 98312 | tf_op jit(solution)/shard_map/ppermute | solution.py:470
  65.4 0.0 collective-permute-done.inside
  65.4 4.2 %collective-permute-done.1.outside = f32[8,8,128]{2,1,0:T(8,128)S(1)} collective-permute-done((f32[8,8,128]{2,1,0:T(8,128)S(1)}, f32[8,8,128]{2,1,0:T(8,128)S(1)}, u32[]{:S(2)}, u32[]{:S(2)}) %collective-permute-start.1) | collective-permute-done | bytes 32800 | tf_op jit(solution)/shard_map/ppermute | solution.py:470
  69.6 0.0 all-to-all-done.3.shared
  69.6 5.5 %shard_map.104 = (f32[8,8,128]{2,1,0:T(8,128)S(1)}, f32[8,8,128]{2,1,0:T(8,128)S(1)}, f32[64,1,128]{2,1,0:T(1,128)}) custom-call(f32[4,64]{1,0:T(4,128)} %bitcast.5, f32[2,4,8,128]{3,2,1,0:T(8,128)} %noise.3, f32[8,128]{1,0:T(8,128)S(1)} %get-tuple-element.25.guidance, f32[8,128]{1,0:T(8,128)S(1)} %get-tuple-element.30.table, ...), custom_call_target="tpu_custom_call" | custom-call | tf_op jit(solution)/shard_map/pallas_call | solution.py:437
  75.1 7.8 %all-to-all-start.4 = ((f32[64,1,128]{2,1,0:T(1,128)}), f32[64,1,128]{2,1,0:T(1,128)S(1)}, u32[]{:S(2)}, u32[]{:S(2)}) async-start(f32[64,1,128]{2,1,0:T(1,128)} %get-tuple-element.42), calls=%async_computation.4 | async-start | bytes 65536 | tf_op jit(solution)/shard_map/all_to_all | solution.py:460
  82.9 1.6 %collective-permute-start.2 = (f32[8,8,128]{2,1,0:T(8,128)S(1)}, f32[8,8,128]{2,1,0:T(8,128)S(1)}, u32[]{:S(2)}, u32[]{:S(2)}) collective-permute-start(f32[8,8,128]{2,1,0:T(8,128)S(1)} %get-tuple-element.44), channel_id=1, source_target_pairs={{0,4},{4,8},{8,12},{12,16},{16,20},{20,24},{24,28},{28,32},{32,36}... | collective-permute-start | bytes 98312 | tf_op jit(solution)/shard_map/ppermute | solution.py:465
  84.6 8.1 %collective-permute-done.2.spill_left = f32[8,8,128]{2,1,0:T(8,128)S(1)} collective-permute-done((f32[8,8,128]{2,1,0:T(8,128)S(1)}, f32[8,8,128]{2,1,0:T(8,128)S(1)}, u32[]{:S(2)}, u32[]{:S(2)}) %collective-permute-start.2) | collective-permute-done | bytes 32800 | tf_op jit(solution)/shard_map/ppermute | solution.py:465
  92.6 2.4 %all-to-all-done.4.squares = f32[64,1,128]{2,1,0:T(1,128)S(1)} async-done(((f32[64,1,128]{2,1,0:T(1,128)}), f32[64,1,128]{2,1,0:T(1,128)S(1)}, u32[]{:S(2)}, u32[]{:S(2)}) %all-to-all-start.4) | async-done | bytes 32800 | tf_op jit(solution)/shard_map/all_to_all | solution.py:460
  95.0 0.8 shard_map.105
Async XLA Ops:
  1.5 18.0 %copy-start.4 = (s32[2]{0:T(128)S(1)}, s32[2]{0:T(128)}, u32[]{:S(2)}) copy-start(s32[2]{0:T(128)} %anchors.3) | copy-start | bytes 28
  20.2 15.6 %copy-start = (bf16[320,320]{1,0:T(8,128)(2,1)S(1)}, bf16[320,320]{1,0:T(8,128)(2,1)}, u32[]{:S(2)}) copy-start(bf16[320,320]{1,0:T(8,128)(2,1)} %w_mid.1) | copy-start | bytes 614404
  20.2 15.6 %copy-start.1 = (bf16[320,36]{0,1:T(8,128)(2,1)S(1)}, bf16[320,36]{0,1:T(8,128)(2,1)}, u32[]{:S(2)}) copy-start(bf16[320,36]{0,1:T(8,128)(2,1)} %param.15) | copy-start | bytes 69124
  20.2 15.6 %copy-start.2 = (bf16[36,320]{1,0:T(8,128)(2,1)S(1)}, bf16[36,320]{1,0:T(8,128)(2,1)}, u32[]{:S(2)}) copy-start(bf16[36,320]{1,0:T(8,128)(2,1)} %w_out.3) | copy-start | bytes 69124
  20.2 15.6 %copy-start.3 = (f32[4,8,128]{2,1,0:T(8,128)S(1)}, f32[4,8,128]{2,1,0:T(8,128)}, u32[]{:S(2)}) copy-start(f32[4,8,128]{2,1,0:T(8,128)} %latent.3) | copy-start | bytes 49156
  55.9 13.7 %all-to-all-start.3 = ((f32[8,9,8,128]{3,2,1,0:T(8,128)}), f32[8,9,8,128]{3,2,1,0:T(8,128)S(1)}, u32[]{:S(2)}, u32[]{:S(2)}) async-start(f32[8,9,8,128]{3,2,1,0:T(8,128)} %shard_map.103), calls=%async_computation.3 | async-start | bytes 589824 | tf_op jit(solution)/shard_map/all_to_all | solution.py:460
  59.4 6.1 %collective-permute-start = (f32[8,8,128]{2,1,0:T(8,128)S(1)}, f32[8,8,128]{2,1,0:T(8,128)S(1)}, u32[]{:S(2)}, u32[]{:S(2)}) collective-permute-start(f32[8,8,128]{2,1,0:T(8,128)S(1)} %get-tuple-element.34), channel_id=1, source_target_pairs={{0,4},{4,0},{8,12},{12,8},{16,20},{20,16},{24,28},{28,24},{32,36},... | collective-permute-start | bytes 98312 | tf_op jit(solution)/shard_map/ppermute | solution.py:470
  60.0 9.6 %collective-permute-start.1 = (f32[8,8,128]{2,1,0:T(8,128)S(1)}, f32[8,8,128]{2,1,0:T(8,128)S(1)}, u32[]{:S(2)}, u32[]{:S(2)}) collective-permute-start(f32[8,8,128]{2,1,0:T(8,128)S(1)} %get-tuple-element.35), channel_id=1, source_target_pairs={{4,8},{8,4},{12,16},{16,12},{20,24},{24,20},{28,32},{32,28},{36,40... | collective-permute-start | bytes 98312 | tf_op jit(solution)/shard_map/ppermute | solution.py:470
  75.1 19.9 %all-to-all-start.4 = ((f32[64,1,128]{2,1,0:T(1,128)}), f32[64,1,128]{2,1,0:T(1,128)S(1)}, u32[]{:S(2)}, u32[]{:S(2)}) async-start(f32[64,1,128]{2,1,0:T(1,128)} %get-tuple-element.42), calls=%async_computation.4 | async-start | bytes 65536 | tf_op jit(solution)/shard_map/all_to_all | solution.py:460
  82.9 9.7 %collective-permute-start.2 = (f32[8,8,128]{2,1,0:T(8,128)S(1)}, f32[8,8,128]{2,1,0:T(8,128)S(1)}, u32[]{:S(2)}, u32[]{:S(2)}) collective-permute-start(f32[8,8,128]{2,1,0:T(8,128)S(1)} %get-tuple-element.44), channel_id=1, source_target_pairs={{0,4},{4,8},{8,12},{12,16},{16,20},{20,24},{24,28},{28,32},{32,36}... | collective-permute-start | bytes 98312 | tf_op jit(solution)/shard_map/ppermute | solution.py:465
